TPU v7x, 16 devices: a whole 2x2x2 slice. The times are simulated.
16 devices in a mesh: tube: 2 (over z), col: 2 (over y), row: 4 (over x, core).
Axes of the slice: x: 2, y: 2, z: 2, core: 2. Of those that a mesh axis runs over, the one named last changes fastest.
Arguments:
- tensor: float32 [32, 1024, 2048], P('tube', 'row', 'col')
- b_init: float32 [2048, 128], P(('col', 'row', 'tube'))
- c_init: float32 [32, 128], replicated
- ridge_lam: float32 [], replicated
Outputs:
- output 1: float32 [1024, 128], P(('row', 'col', 'tube'))
- output 2: float32 [2048, 128], P(('col', 'row', 'tube'))
- output 3: float32 [32, 128], replicated
All inputs are finite; a program needn't handle non-finite values.
Results may differ from a plain program's by a relative error of at most 0.001.
Values are sent between devices in bfloat16 or wider.
A program may use at most 1 GiB of HBM per device.

v0:
```python
import jax
import jax.numpy as jnp
from jax import lax
from jax.sharding import PartitionSpec as P, NamedSharding

SWEEPS = 2
ALL_AXES = ("tube", "col", "row")


def gram_of(factor):
    half_fac = factor.astype(jnp.bfloat16)
    return lax.dot_general(half_fac, half_fac, (((0,), (0,)), ((), ())), preferred_element_type=jnp.float32)


def solve_rows(mttkrp_rows, gram_prod, ridge_lam):
    ident_mat = jnp.eye(gram_prod.shape[0], dtype=jnp.float32)
    chol_fac = jnp.linalg.cholesky(gram_prod + ridge_lam * ident_mat)
    half_solve = lax.linalg.triangular_solve(chol_fac, mttkrp_rows, left_side=False, lower=True, transpose_a=True)
    return lax.linalg.triangular_solve(chol_fac, half_solve, left_side=False, lower=True)


def solution(mesh):
    full_prec = lax.Precision.HIGHEST

    def local_sweeps(x_blk, b_own, c_full, ridge_lam):
        k_loc, i_loc, j_loc = x_blk.shape
        cp_rank = b_own.shape[1]
        x_half = x_blk.astype(jnp.bfloat16)
        flat_x = x_half.reshape(k_loc * i_loc, j_loc)
        tube_idx = lax.axis_index("tube")
        b_cols = lax.all_gather(b_own, ("row", "tube"), axis=0, tiled=True)
        gram_b = lax.psum(gram_of(b_own), ALL_AXES)
        for sweep_idx in range(SWEEPS):
            c_blk = lax.dynamic_slice_in_dim(c_full, tube_idx * k_loc, k_loc, 0)
            gram_c = gram_of(c_full)
            u_kir = jnp.dot(flat_x, b_cols.astype(jnp.bfloat16), preferred_element_type=jnp.float32).reshape(k_loc, i_loc, cp_rank)
            part_a = jnp.einsum("kir,kr->ir", u_kir, c_blk, preferred_element_type=jnp.float32, precision=full_prec)
            mtt_a = lax.psum_scatter(part_a, ("col", "tube"), scatter_dimension=0, tiled=True)
            a_own = solve_rows(mtt_a, gram_b * gram_c, ridge_lam)
            gram_a = lax.psum(gram_of(a_own), ALL_AXES)
            a_rows = lax.all_gather(a_own, ("col", "tube"), axis=0, tiled=True)
            v_kjr = jnp.einsum("kij,ir->kjr", x_half, a_rows.astype(jnp.bfloat16), preferred_element_type=jnp.float32)
            part_b = jnp.einsum("kjr,kr->jr", v_kjr, c_blk, preferred_element_type=jnp.float32, precision=full_prec)
            mtt_b = lax.psum_scatter(part_b, ("row", "tube"), scatter_dimension=0, tiled=True)
            b_own = solve_rows(mtt_b, gram_a * gram_c, ridge_lam)
            gram_b = lax.psum(gram_of(b_own), ALL_AXES)
            b_cols = lax.all_gather(b_own, ("row", "tube"), axis=0, tiled=True)
            u_kir = jnp.dot(flat_x, b_cols.astype(jnp.bfloat16), preferred_element_type=jnp.float32).reshape(k_loc, i_loc, cp_rank)
            part_c = jnp.einsum("kir,ir->kr", u_kir, a_rows, preferred_element_type=jnp.float32, precision=full_prec)
            c_local = lax.psum(part_c, ("row", "col"))
            mtt_c = lax.all_gather(c_local, "tube", axis=0, tiled=True)
            c_full = solve_rows(mtt_c, gram_a * gram_b, ridge_lam)
        return a_own, b_own, c_full

    return jax.shard_map(
        local_sweeps,
        mesh=mesh,
        in_specs=(P("tube", "row", "col"), P(("col", "row", "tube"), None), P(None, None), P()),
        out_specs=(P(("row", "col", "tube"), None), P(("col", "row", "tube"), None), P(None, None)),
        check_vma=False,
    )
```

profile of v0, /device:TPU:0, one launch (start us, length us, event | category | flops | bytes accessed | tf_op | source)
XLA Modules:
  0.0 596.3 jit_solution(18042775992400540972)
XLA Ops:
  8.0 1.8 fusion.52
  9.9 0.8 convert
  10.7 9.1 %convert_element_type.48 = bf16[16,256,1024]{2,1,0:T(8,128)(2,1)} convert(f32[16,256,1024]{2,1,0:T(8,128)} %param.17) | non-fusion elementwise | flops 4194304 | bytes 25165824 | tf_op jit(solution)/shard_map/convert_element_type | solution.py:28
  19.8 18.4 %all_gather.21 = bf16[1024,128]{1,0:T(8,128)(2,1)S(1)} all-gather(bf16[128,128]{1,0:T(8,128)(2,1)S(1)} %convert), channel_id=1, replica_groups=mesh['tube'=2,'col'=2,'row'=4] {'row','tube'}, dimensions={0}, use_global_device_ids=true | all-gather | bytes 294912 | tf_op jit(solution)/shard_map/all_gather | solution.py:31
  38.2 6.4 %multiply_reduce_fusion.2 = f32[128,256]{0,1:T(8,128)} fusion(bf16[16,256,1024]{2,1,0:T(8,128)(2,1)} %convert_element_type.48, f32[128,16]{0,1:T(8,128)S(1)} %get-tuple-element.16, bf16[1024,128]{1,0:T(8,128)(2,1)S(1)} %all_gather.21), kind=kOutput, calls=%fused_computation.8 | convolution fusion | flops 1074757632 | bytes 8790016 | tf_op jit(solution)/shard_map/dot_general | solution.py:36
  45.4 35.9 %all-reduce.6.cloned.1.call-done = f32[128,128]{0,1:T(8,128)} async-done(((f32[128,128]{0,1:T(8,128)}), f32[128,128]{0,1:T(8,128)}) %all-reduce.6.cloned.1.call-update) | async-done | bytes 65552 | tf_op jit(solution)/shard_map/psum | solution.py:32
  81.4 1.1 select_add_fusion.5
  82.5 11.7 %cholesky.104 = f32[128,128]{1,0:T(8,128)S(1)} custom-call(f32[128,128]{1,0:T(8,128)S(1)} %fusion.39), custom_call_target="Cholesky" | custom-call | tf_op jit(solution)/shard_map/jit(cholesky)/cholesky | solution.py:17
  94.9 0.7 fusion.12
  95.6 9.8 %custom-call.27 = f32[1,128,128]{1,2,0:T(8,128)S(1)} custom-call(f32[1,128,128]{2,1,0:T(8,128)S(1)} %fusion.12), custom_call_target="InvertDiagBlocksLowerTriangular" | custom-call | tf_op jit(solution)/shard_map/triangular_solve/custom-call.2 | solution.py:19
  105.4 1.0 convolution_bitcast_fusion.7
  106.8 7.5 %all_gather.22 = f32[256,128]{1,0:T(8,128)S(1)} all-gather(f32[64,128]{1,0:T(8,128)S(1)} %convolution_bitcast_fusion.9), channel_id=1, replica_groups=mesh['tube'=2,'col'=2,'row'=4] {'col','tube'}, dimensions={0}, use_global_device_ids=true | all-gather | bytes 163840 | tf_op jit(solution)/shard_map/all_gather | solution.py:41
  114.3 0.8 fusion.56
  115.1 7.9 %fusion.32 = f32[128,16,1024]{2,0,1:T(8,128)} fusion(bf16[16,256,1024]{2,1,0:T(8,128)(2,1)} %convert_element_type.48, f32[256,128]{1,0:T(8,128)S(1)} %all_gather.22), kind=kOutput, calls=%fused_computation.65 | convolution fusion | flops 1073774592 | bytes 16908288 | tf_op jit(solution)/shard_map/kij,ir->kjr/dot_general | solution.py:42
  123.3 12.6 %fusion.2 = f32[128,1,1024]{2,1,0:T(1,128)S(1)} fusion(f32[16,128,1]{0,2,1:T(1,128)S(1)} %copy.50, f32[128,16,1024]{2,0,1:T(8,128)} %fusion.32), kind=kOutput, calls=%fused_computation.2 | convolution fusion | flops 25165824 | bytes 8921088 | tf_op jit(solution)/shard_map/kjr,kr->jr/dot_general | solution.py:43
  135.9 0.9 copy.94
  137.0 50.4 %all-reduce.8.cloned.1.call-done = f32[128,128]{0,1:T(8,128)} async-done(((f32[128,128]{0,1:T(8,128)}), f32[128,128]{0,1:T(8,128)}) %all-reduce.8.cloned.1.call-update) | async-done | bytes 65552 | tf_op jit(solution)/shard_map/psum | solution.py:40
  187.5 0.9 select_add_fusion.4
  188.4 11.7 %cholesky.115 = f32[128,128]{1,0:T(8,128)S(1)} custom-call(f32[128,128]{1,0:T(8,128)S(1)} %fusion.36), custom_call_target="Cholesky" | custom-call | tf_op jit(solution)/shard_map/jit(cholesky)/cholesky | solution.py:17
  200.8 0.7 fusion.13
  201.5 9.8 %custom-call.29 = f32[1,128,128]{1,2,0:T(8,128)S(1)} custom-call(f32[1,128,128]{2,1,0:T(8,128)S(1)} %fusion.13), custom_call_target="InvertDiagBlocksLowerTriangular" | custom-call | tf_op jit(solution)/shard_map/triangular_solve/custom-call.4 | solution.py:19
  211.3 6.4 %reduce-scatter.9.cloned.1.call-done = f32[128,128]{0,1:T(8,128)} async-done(((f32[1024,128]{0,1:T(8,128)}), f32[128,128]{0,1:T(8,128)}) %reduce-scatter.9.cloned.1.call-update) | async-done | bytes 65552 | tf_op jit(solution)/shard_map/reduce_scatter | solution.py:44
  217.7 1.1 convolution_bitcast_fusion.6
  219.1 17.1 %all_gather.23 = bf16[1024,128]{0,1:T(8,128)(2,1)S(1)} all-gather(bf16[128,128]{0,1:T(8,128)(2,1)S(1)} %convolution_bitcast_fusion.5), channel_id=1, replica_groups=mesh['tube'=2,'col'=2,'row'=4] {'row','tube'}, dimensions={0}, use_global_device_ids=true | all-gather | bytes 294912 | tf_op jit(solution)/shard_map/all_gather | solution.py:47
  236.2 0.8 fusion.66
  237.0 6.3 %fusion.65 = f32[128,4096]{1,0:T(8,128)S(1)} fusion(bf16[1024,128]{0,1:T(8,128)(2,1)S(1)} %all_gather.23, bf16[4096,1024]{1,0:T(8,128)(2,1)} %bitcast.189), kind=kOutput, calls=%fused_computation.115 | convolution fusion | flops 1073741824 | bytes 10747904 | tf_op jit(solution)/shard_map/dot_general | solution.py:48
  243.2 0.7 copy.81
  244.4 13.8 %psum.52 = f32[16,128]{1,0:T(8,128)S(1)} all-reduce(f32[16,128]{1,0:T(8,128)S(1)} %bitcast.202), channel_id=1, replica_groups=mesh['tube'=2,'col'=2,'row'=4] {'row','col'}, use_global_device_ids=true, to_apply=%region_7.13 | all-reduce | flops 2048 | bytes 16384 | tf_op jit(solution)/shard_map/psum | solution.py:50
  258.2 4.8 all_gather.24
  262.9 46.1 %all-reduce.10.cloned.1.call-done = f32[128,128]{0,1:T(8,128)} async-done(((f32[128,128]{0,1:T(8,128)}), f32[128,128]{0,1:T(8,128)}) %all-reduce.10.cloned.1.call-update) | async-done | bytes 65552 | tf_op jit(solution)/shard_map/psum | solution.py:46
  309.0 0.9 select_add_fusion.3
  310.0 11.7 %cholesky.126 = f32[128,128]{1,0:T(8,128)S(1)} custom-call(f32[128,128]{1,0:T(8,128)S(1)} %fusion.31), custom_call_target="Cholesky" | custom-call | tf_op jit(solution)/shard_map/jit(cholesky)/cholesky | solution.py:17
  322.4 0.7 fusion.14
  323.1 9.8 %custom-call.31 = f32[1,128,128]{1,2,0:T(8,128)S(1)} custom-call(f32[1,128,128]{2,1,0:T(8,128)S(1)} %fusion.14), custom_call_target="InvertDiagBlocksLowerTriangular" | custom-call | tf_op jit(solution)/shard_map/triangular_solve/custom-call.6 | solution.py:19
  333.6 1.2 fusion.63
  334.8 0.8 copy.77
  335.8 1.1 select_add_fusion.2
  336.9 11.7 %cholesky.137 = f32[128,128]{1,0:T(8,128)S(1)} custom-call(f32[128,128]{1,0:T(8,128)S(1)} %fusion.28), custom_call_target="Cholesky" | custom-call | tf_op jit(solution)/shard_map/jit(cholesky)/cholesky | solution.py:17
  349.3 0.7 fusion.15
  350.0 9.8 %custom-call.33 = f32[1,128,128]{1,2,0:T(8,128)S(1)} custom-call(f32[1,128,128]{2,1,0:T(8,128)S(1)} %fusion.15), custom_call_target="InvertDiagBlocksLowerTriangular" | custom-call | tf_op jit(solution)/shard_map/triangular_solve/custom-call.2 | solution.py:19
  359.8 1.0 convolution_bitcast_fusion.3
  361.2 7.5 %all_gather.25 = f32[256,128]{1,0:T(8,128)S(1)} all-gather(f32[64,128]{1,0:T(8,128)S(1)} %convolution_bitcast_fusion.8), channel_id=1, replica_groups=mesh['tube'=2,'col'=2,'row'=4] {'col','tube'}, dimensions={0}, use_global_device_ids=true | all-gather | bytes 163840 | tf_op jit(solution)/shard_map/all_gather | solution.py:41
  368.7 0.8 fusion.54
  369.5 7.9 %fusion.21 = f32[128,16,1024]{2,0,1:T(8,128)} fusion(bf16[16,256,1024]{2,1,0:T(8,128)(2,1)} %convert_element_type.48, f32[256,128]{1,0:T(8,128)S(1)} %all_gather.25), kind=kOutput, calls=%fused_computation.51 | convolution fusion | flops 1073774592 | bytes 16908288 | tf_op jit(solution)/shard_map/kij,ir->kjr/dot_general | solution.py:42
  377.7 12.6 %fusion = f32[128,1,1024]{2,1,0:T(1,128)S(1)} fusion(f32[16,128,1]{0,2,1:T(1,128)S(1)} %copy.60, f32[128,16,1024]{2,0,1:T(8,128)} %fusion.21), kind=kOutput, calls=%fused_computation | convolution fusion | flops 25165824 | bytes 8921088 | tf_op jit(solution)/shard_map/kjr,kr->jr/dot_general | solution.py:43
  390.3 0.9 copy.93
  391.7 50.2 %all-reduce.12.cloned.1.call-done = f32[128,128]{0,1:T(8,128)} async-done(((f32[128,128]{0,1:T(8,128)}), f32[128,128]{0,1:T(8,128)}) %all-reduce.12.cloned.1.call-update) | async-done | bytes 65552 | tf_op jit(solution)/shard_map/psum | solution.py:40
  441.9 0.9 select_add_fusion.1
  442.8 11.7 %cholesky.148 = f32[128,128]{1,0:T(8,128)S(1)} custom-call(f32[128,128]{1,0:T(8,128)S(1)} %fusion.25), custom_call_target="Cholesky" | custom-call | tf_op jit(solution)/shard_map/jit(cholesky)/cholesky | solution.py:17
  455.9 9.8 %custom-call.35 = f32[1,128,128]{1,2,0:T(8,128)S(1)} custom-call(f32[1,128,128]{2,1,0:T(8,128)S(1)} %fusion.16), custom_call_target="InvertDiagBlocksLowerTriangular" | custom-call | tf_op jit(solution)/shard_map/triangular_solve/custom-call.4 | solution.py:19
  465.7 6.3 %reduce-scatter.11.cloned.1.call-done = f32[128,128]{0,1:T(8,128)} async-done(((f32[1024,128]{0,1:T(8,128)}), f32[128,128]{0,1:T(8,128)}) %reduce-scatter.11.cloned.1.call-update) | async-done | bytes 65552 | tf_op jit(solution)/shard_map/reduce_scatter | solution.py:44
  472.0 1.1 convolution_bitcast_fusion.2
  473.3 17.1 %all_gather.26 = bf16[1024,128]{0,1:T(8,128)(2,1)S(1)} all-gather(bf16[128,128]{0,1:T(8,128)(2,1)S(1)} %get-tuple-element.22), channel_id=1, replica_groups=mesh['tube'=2,'col'=2,'row'=4] {'row','tube'}, dimensions={0}, use_global_device_ids=true | all-gather | bytes 294912 | tf_op jit(solution)/shard_map/all_gather | solution.py:47
  490.5 6.3 %fusion.64 = f32[128,4096]{1,0:T(8,128)S(1)} fusion(bf16[1024,128]{0,1:T(8,128)(2,1)S(1)} %all_gather.26, bf16[4096,1024]{1,0:T(8,128)(2,1)} %bitcast.190), kind=kOutput, calls=%fused_computation.114 | convolution fusion | flops 1073741824 | bytes 10747904 | tf_op jit(solution)/shard_map/dot_general | solution.py:48
  496.7 0.7 copy.82
  497.4 0.8 fusion.48
  498.6 0.7 copy.38
  499.4 13.8 %psum.55 = f32[16,128]{1,0:T(8,128)S(1)} all-reduce(f32[16,128]{1,0:T(8,128)S(1)} %bitcast.203), channel_id=1, replica_groups=mesh['tube'=2,'col'=2,'row'=4] {'row','col'}, use_global_device_ids=true, to_apply=%region_12.20 | all-reduce | flops 2048 | bytes 16384 | tf_op jit(solution)/shard_map/psum | solution.py:50
  513.1 4.7 all_gather.27
  517.8 45.5 %all-reduce.14.cloned.1.call-done = f32[128,128]{0,1:T(8,128)} async-done(((f32[128,128]{0,1:T(8,128)}), f32[128,128]{0,1:T(8,128)}) %all-reduce.14.cloned.1.call-update) | async-done | bytes 65552 | tf_op jit(solution)/shard_map/psum | solution.py:46
  563.3 0.9 select_add_fusion
  564.3 11.7 %cholesky.159 = f32[128,128]{1,0:T(8,128)S(1)} custom-call(f32[128,128]{1,0:T(8,128)S(1)} %fusion.20), custom_call_target="Cholesky" | custom-call | tf_op jit(solution)/shard_map/jit(cholesky)/cholesky | solution.py:17
  577.4 9.8 %custom-call.37 = f32[1,128,128]{1,2,0:T(8,128)S(1)} custom-call(f32[1,128,128]{2,1,0:T(8,128)S(1)} %fusion.17), custom_call_target="InvertDiagBlocksLowerTriangular" | custom-call | tf_op jit(solution)/shard_map/triangular_solve/custom-call.6 | solution.py:19
  587.5 0.9 convolution_bitcast_fusion.10
  (71 shorter events, 10.4 us)
Async XLA Ops:
  8.0 73.4 %all-reduce.6.cloned.1.call-start = ((), (), s32[]{:S(2)}) async-start(), calls=%async_computation.4 | async-start | bytes 131072 | tf_op jit(solution)/shard_map/psum | solution.py:32
  9.8 95.6 %reduce-scatter.13.cloned.1.call-start = ((), (), s32[]{:S(2)}) async-start(), calls=%async_computation.11 | async-start | bytes 163840
  10.7 27.5 %copy-start.3 = (f32[32,128]{1,0:T(8,128)S(1)}, f32[32,128]{1,0:T(8,128)}, u32[]{:S(2)}) copy-start(f32[32,128]{1,0:T(8,128)} %param.19) | copy-start | bytes 49156
  44.6 142.8 %all-reduce.8.cloned.1.call-start = ((), (), s32[]{:S(2)}) async-start(), calls=%async_computation.5 | async-start | bytes 131072 | tf_op jit(solution)/shard_map/psum | solution.py:40
  123.0 94.7 %reduce-scatter.9.cloned.1.call-start = ((), (), s32[]{:S(2)}) async-start(), calls=%async_computation.6 | async-start | bytes 589824 | tf_op jit(solution)/shard_map/reduce_scatter | solution.py:44
  137.0 172.1 %all-reduce.10.cloned.1.call-start = ((), (), s32[]{:S(2)}) async-start(), calls=%async_computation.7 | async-start | bytes 131072 | tf_op jit(solution)/shard_map/psum | solution.py:46
  237.0 72.1 %copy-start.2 = (f32[128,128]{0,1:T(8,128)S(1)}, f32[128,128]{0,1:T(8,128)}, u32[]{:S(2)}) copy-start(f32[128,128]{0,1:T(8,128)} %all-reduce.8.cloned.1.call-done) | copy-start | bytes 196612
  243.9 115.9 %reduce-scatter.15.cloned.1.call-start = ((), (), s32[]{:S(2)}) async-start(), calls=%async_computation.12 | async-start | bytes 163840
  335.5 106.3 %all-reduce.12.cloned.1.call-start = ((), (), s32[]{:S(2)}) async-start(), calls=%async_computation.8 | async-start | bytes 131072 | tf_op jit(solution)/shard_map/psum | solution.py:40
  361.2 16.3 %copy-start = (f32[64,128]{1,0:T(8,128)}, f32[64,128]{1,0:T(8,128)S(1)}, u32[]{:S(2)}) copy-start(f32[64,128]{1,0:T(8,128)S(1)} %convolution_bitcast_fusion.8) | copy-start | bytes 98308
  377.5 94.6 %reduce-scatter.11.cloned.1.call-start = ((), (), s32[]{:S(2)}) async-start(), calls=%async_computation.9 | async-start | bytes 589824 | tf_op jit(solution)/shard_map/reduce_scatter | solution.py:44
  391.4 171.9 %all-reduce.14.cloned.1.call-start = ((), (), s32[]{:S(2)}) async-start(), calls=%async_computation.10 | async-start | bytes 131072 | tf_op jit(solution)/shard_map/psum | solution.py:46
  490.5 72.9 %copy-start.1 = (f32[128,128]{0,1:T(8,128)S(1)}, f32[128,128]{0,1:T(8,128)}, u32[]{:S(2)}) copy-start(f32[128,128]{0,1:T(8,128)} %all-reduce.12.cloned.1.call-done) | copy-start | bytes 196612
Sparse Core Ops, SparseCore 0:
  13.6 67.7 all-reduce.5
  123.1 64.2 all-reduce.7
  190.5 27.1 reduce-scatter.8
  244.1 64.9 all-reduce.9
  377.6 64.2 all-reduce.11
  444.8 27.1 reduce-scatter.10
  498.3 64.9 all-reduce.13
Sparse Core Ops, SparseCore 1:
  44.7 20.7 reduce-scatter.12
  335.6 19.2 reduce-scatter.14
where the time goes:
time: 605 us; the launch traced here: 596 us
  waiting for transfers between devices  241 us (40%)
  other arithmetic  151 us (25%)
  blocking collectives  105 us (17%)
  matrix products  75.2 us (12%)
  between operations  17.2 us (3%)
    psum x3, waiting for transfers between devices, local_sweeps(): gram_b = lax.psum(gram_of(b_own), ALL_AXES)  128 us
    psum x2, waiting for transfers between devices, local_sweeps(): gram_a = lax.psum(gram_of(a_own), ALL_AXES)  101 us
    another operation x18, other arithmetic, solve_rows(): chol_fac = jnp.linalg.cholesky(gram_prod + ridge_lam * ident_mat)  74.3 us
    another operation x12, other arithmetic, solve_rows(): lax.linalg.triangular_solve(chol_fac, half_solve, left_side=False, lower=...  62.8 us
    all_gather x3, blocking collectives, local_sweeps(): b_cols = lax.all_gather(b_own, ('row', 'tube'), axis=0, tiled=True)  52.6 us
    psum x2, blocking collectives, local_sweeps(): c_local = lax.psum(part_c, ('row', 'col'))  27.5 us
    dot_general x2, matrix products, local_sweeps(): jnp.einsum('kjr,kr->jr', v_kjr, c_blk, preferred_element_type=jnp.float32...  25.2 us
    dot_general x3, matrix products, local_sweeps(): jnp.dot(flat_x, b_cols.astype(jnp.bfloat16), preferred_element_type=jnp.f...  18.9 us
  transfers between devices with their start and end apart: 9, of which 7 were waited for; matrix products, arithmetic and copies ran while one was open for 24% of the time, Pallas kernels for 0%

commit v1 on v0

v1 whole, which is shorter than its diff:
```python
import jax
import jax.numpy as jnp
from jax import lax
from jax.experimental import pallas as pl
from jax.experimental.pallas import tpu as pltpu
from jax.sharding import PartitionSpec as P

SWEEPS = 2
HI = lax.Precision.HIGHEST
MESH = pl.DeviceIdType.MESH
F32 = jnp.float32
BF16 = jnp.bfloat16

OFF_YZ = [(t, c, 0) for c in range(2) for t in range(2)][1:]
OFF_XZ = [(t, 0, w) for w in range(4) for t in range(2)][1:]
OFF_ALL_REST = [(t, c, w) for w in range(1, 4) for c in range(2) for t in range(2)]
OFF_ALL = OFF_YZ + OFF_ALL_REST


def dot_t0(a, b, **kw):
    return lax.dot_general(a, b, (((0,), (0,)), ((), ())), preferred_element_type=F32, **kw)


def kernel(
    x_hbm, b_ref, c_ref, lam_ref,
    a_out, b_out, c_out,
    xf, xh, u_ref, bcols, a16, at_ref, af, pa, rsa, vt, rsb, gbp, gbr, pc, cb,
    w_ref, q_ref, li_ref, inv_ref, ga_ref, gb_ref, cfac,
    x_sem, rsa_s, rsa_r, aga_s, aga_r, af_s, af_r, rsb_s, rsb_r, agb_s, agb_r, gb_s, gb_r, pc_s, pc_r,
):
    t = lax.axis_index("tube")
    c = lax.axis_index("col")
    w = lax.axis_index("row")
    kk, ii, jj = xf.shape
    rank = b_ref.shape[1]
    g = c * 2 + t
    q = w * 2 + t
    me = g * 4 + w

    for k in range(kk):
        pltpu.make_async_copy(x_hbm.at[k], xf.at[k], x_sem.at[k]).start()

    def dev(off):
        return ((t + off[0]) % 2, (c + off[1]) % 2, (w + off[2]) % 4)

    barrier = pltpu.get_barrier_semaphore()
    for off in OFF_ALL:
        pl.semaphore_signal(barrier, inc=1, device_id=dev(off), device_id_type=MESH)
    pl.semaphore_wait(barrier, len(OFF_ALL))

    def push(src, dst, ss, rs, off):
        return pltpu.make_async_remote_copy(
            src_ref=src, dst_ref=dst, send_sem=ss, recv_sem=rs, device_id=dev(off), device_id_type=MESH
        )

    def gather_b(s):
        return [
            push(bcols.at[s, q], bcols.at[s, q], agb_s.at[s, n], agb_r.at[s, n], off)
            for n, off in enumerate(OFF_XZ)
        ]

    def gram_copy(s):
        return push(gbp, gbr.at[s], gb_s.at[s], gb_r.at[s], (0, 1, 0))

    def u_pass(s):
        bmat = bcols[s].reshape(jj, rank)

        def body(k, _):
            u_ref[k] = jnp.dot(xh[k], bmat, preferred_element_type=F32)
            return 0

        lax.fori_loop(0, kk, body, 0)

    def start_gram_b(s):
        bmat = bcols[s].reshape(jj, rank)
        gbp[...] = dot_t0(bmat, bmat)
        gram_copy(s).start()

    def finish_gram_b(s):
        gram_copy(s).wait()
        gb_ref[...] = gbp[...] + gbr[s]

    def factor(gram_prod):
        rows = lax.broadcasted_iota(jnp.int32, (rank, rank), 0)
        cols = lax.broadcasted_iota(jnp.int32, (rank, rank), 1)
        eye = jnp.where(rows == cols, 1.0, 0.0).astype(F32)
        w_ref[:, :rank] = gram_prod + lam_ref[0, 0] * eye
        w_ref[:, rank:] = eye
        q_ref[...] = jnp.zeros_like(q_ref)
        r1 = lax.broadcasted_iota(jnp.int32, (8, rank), 0)
        r2 = lax.broadcasted_iota(jnp.int32, (8, 2 * rank), 0)

        def body(b, _):
            off = pl.multiple_of(b * 8, 8)
            pan = w_ref[pl.ds(off, 8), :]
            rolled = pltpu.roll(pan[:, :rank], rank - off, axis=1)
            e = [jnp.broadcast_to(rolled[:, n : n + 1], (8, rank)) for n in range(8)]
            chol = jnp.zeros_like(pan)
            for j in range(8):
                piv = jnp.broadcast_to(e[j][j : j + 1], (8, rank))
                isq = lax.rsqrt(piv)
                rc = isq * isq
                m = e[j] * rc
                m2 = jnp.concatenate([m, m], axis=1)
                isq2 = jnp.concatenate([isq, isq], axis=1)
                rc2 = jnp.concatenate([rc, rc], axis=1)
                pj = jnp.broadcast_to(pan[j : j + 1], (8, 2 * rank))
                chol = jnp.where(r2 == j, pj * isq2, chol)
                pan = jnp.where(r2 == j, pj * rc2, pan - m2 * pj)
                for n in range(j + 1, 8):
                    en = jnp.broadcast_to(e[n][j : j + 1], (8, rank))
                    e[n] = jnp.where(r1 == j, en * rc, e[n] - m * en)
            li_ref[pl.ds(off, 8), :] = chol[:, rank:]
            q_ref[pl.ds(off, 8), :] = pan
            w_ref[...] = w_ref[...] - jnp.dot(w_ref[:, :rank], q_ref[...], precision=HI, preferred_element_type=F32)
            q_ref[pl.ds(off, 8), :] = jnp.zeros_like(pan)
            return 0

        lax.fori_loop(0, rank // 8, body, 0)
        inv_ref[...] = dot_t0(li_ref[...], li_ref[...], precision=HI)

    bcols[0, q] = b_ref[...].astype(BF16)
    cps = gather_b(0)
    for cp in cps:
        cp.start()
    cfac[...] = c_ref[...]

    def load(k, _):
        pltpu.make_async_copy(x_hbm.at[k], xf.at[k], x_sem.at[k]).wait()
        xh[k] = xf[k].astype(BF16)
        return 0

    lax.fori_loop(0, kk, load, 0)
    for cp in cps:
        cp.wait()
    start_gram_b(0)
    u_pass(0)
    finish_gram_b(0)

    def sweep(s, _):
        c16 = cfac[...].astype(BF16)
        gram_c = dot_t0(c16, c16)

        def body_a(k, acc):
            return acc + u_ref[k] * cfac[pl.ds(t * kk + k, 1), :]

        part = lax.fori_loop(0, kk, body_a, jnp.zeros((ii, rank), F32))
        pa[...] = part.reshape(pa.shape)
        ra = []
        for n, off in enumerate(OFF_YZ):
            g2 = dev(off)[1] * 2 + dev(off)[0]
            ra.append(push(pa.at[g2], rsa.at[s, n], rsa_s.at[s, n], rsa_r.at[s, n], off))
        for cp in ra:
            cp.start()
        factor(gb_ref[...] * gram_c)
        for cp in ra:
            cp.wait()
        mtt_a = pa[g] + rsa[s, 0] + rsa[s, 1] + rsa[s, 2]
        a_own = jnp.dot(mtt_a, inv_ref[...], precision=HI, preferred_element_type=F32)
        a_out[...] = a_own
        a16[s, w, g] = a_own.astype(BF16)
        af[s, g] = a_own
        ga = [push(a16.at[s, w, g], a16.at[s, w, g], aga_s.at[s, n], aga_r.at[s, n], off) for n, off in enumerate(OFF_ALL)]
        for cp in ga:
            cp.start()
        fa = [push(af.at[s, g], af.at[s, g], af_s.at[s, n], af_r.at[s, n], off) for n, off in enumerate(OFF_YZ)]
        for cp in fa:
            cp.start()

        cmine = cfac[pl.ds(pl.multiple_of(t * kk, kk), kk), :]
        ct = jnp.transpose(jnp.concatenate([cmine, jnp.zeros((rank - kk, rank), F32)], axis=0))
        for k in range(kk):
            cb[k] = jnp.broadcast_to(ct[:, k : k + 1], (rank, rank))
        for cp in ga[:3]:
            cp.wait()
        at_ref[...] = jnp.transpose(a16[s, w].reshape(ii, rank))
        vt[...] = jnp.zeros_like(vt)

        def body_b(k, _):
            v = jnp.dot(at_ref[...], xh[k], preferred_element_type=F32)
            ck = cb[k]
            for n in range(jj // rank):
                vt[n] += v[:, n * rank : (n + 1) * rank] * ck
            return 0

        lax.fori_loop(0, kk, body_b, 0)
        rb = []
        for n, off in enumerate(OFF_XZ):
            q2 = dev(off)[2] * 2 + dev(off)[0]
            rb.append(push(vt.at[q2], rsb.at[s, n], rsb_s.at[s, n], rsb_r.at[s, n], off))
        for cp in rb:
            cp.start()
        for cp in ga[3:]:
            cp.wait()
        aall = a16[s].reshape(4 * ii, rank)
        ga_ref[...] = dot_t0(aall, aall)
        factor(ga_ref[...] * gram_c)
        for cp in rb:
            cp.wait()
        mtt_b = vt[q]
        for n in range(len(OFF_XZ)):
            mtt_b = mtt_b + rsb[s, n]
        b_own = jnp.transpose(jnp.dot(inv_ref[...], mtt_b, precision=HI, preferred_element_type=F32))
        b_out[...] = b_own
        bcols[s + 1, q] = b_own.astype(BF16)
        gcs = gather_b(s + 1)
        for cp in gcs:
            cp.start()
        for cp in gcs:
            cp.wait()

        start_gram_b(s + 1)
        u_pass(s + 1)
        for cp in fa:
            cp.wait()
        afull = af[s].reshape(ii, rank)
        pc[s, me] = jnp.concatenate(
            [jnp.sum(u_ref[k] * afull, axis=0, keepdims=True) for k in range(kk)], axis=0
        )
        cs = [push(pc.at[s, me], pc.at[s, me], pc_s.at[s, n], pc_r.at[s, n], off) for n, off in enumerate(OFF_ALL)]
        for cp in cs:
            cp.start()
        finish_gram_b(s + 1)
        factor(ga_ref[...] * gb_ref[...])
        for cp in cs:
            cp.wait()
        halves = []
        for t2 in range(2):
            tot = None
            for c2 in range(2):
                for w2 in range(4):
                    term = pc[s, (c2 * 2 + t2) * 4 + w2]
                    tot = term if tot is None else tot + term
            halves.append(tot)
        cfac[...] = jnp.dot(jnp.concatenate(halves, axis=0), inv_ref[...], precision=HI, preferred_element_type=F32)
        return 0

    lax.fori_loop(0, SWEEPS, sweep, 0)
    c_out[...] = cfac[...]


def solution(mesh):
    def local_sweeps(x_blk, b_own, c_full, ridge_lam):
        kk, ii, jj = x_blk.shape
        rank = b_own.shape[1]
        arows, brows = ii // 4, b_own.shape[0]
        dma = pltpu.SemaphoreType.DMA
        vmem = pl.BlockSpec(memory_space=pltpu.VMEM)
        return pl.pallas_call(
            kernel,
            name="als",
            out_shape=(
                jax.ShapeDtypeStruct((arows, rank), F32),
                jax.ShapeDtypeStruct((brows, rank), F32),
                jax.ShapeDtypeStruct(c_full.shape, F32),
            ),
            in_specs=[
                pl.BlockSpec(memory_space=pl.ANY), vmem, vmem, pl.BlockSpec(memory_space=pltpu.SMEM),
            ],
            out_specs=(vmem, vmem, vmem),
            scratch_shapes=[
                pltpu.VMEM((kk, ii, jj), F32),
                pltpu.VMEM((kk, ii, jj), BF16),
                pltpu.VMEM((kk, ii, rank), F32),
                pltpu.VMEM((SWEEPS + 1, 8, brows, rank), BF16),
                pltpu.VMEM((SWEEPS, 4, 4, arows, rank), BF16),
                pltpu.VMEM((rank, ii), BF16),
                pltpu.VMEM((SWEEPS, 4, arows, rank), F32),
                pltpu.VMEM((4, arows, rank), F32),
                pltpu.VMEM((SWEEPS, 3, arows, rank), F32),
                pltpu.VMEM((8, rank, brows), F32),
                pltpu.VMEM((SWEEPS, 7, rank, brows), F32),
                pltpu.VMEM((rank, rank), F32),
                pltpu.VMEM((SWEEPS + 1, rank, rank), F32),
                pltpu.VMEM((SWEEPS, 16, kk, rank), F32),
                pltpu.VMEM((kk, rank, rank), F32),
                pltpu.VMEM((rank, 2 * rank), F32),
                pltpu.VMEM((rank, 2 * rank), F32),
                pltpu.VMEM((rank, rank), F32),
                pltpu.VMEM((rank, rank), F32),
                pltpu.VMEM((rank, rank), F32),
                pltpu.VMEM((rank, rank), F32),
                pltpu.VMEM(c_full.shape, F32),
                dma((kk,)),
                dma((SWEEPS, 3)), dma((SWEEPS, 3)),
                dma((SWEEPS, 15)), dma((SWEEPS, 15)),
                dma((SWEEPS, 3)), dma((SWEEPS, 3)),
                dma((SWEEPS, 7)), dma((SWEEPS, 7)),
                dma((SWEEPS + 1, 7)), dma((SWEEPS + 1, 7)),
                dma((SWEEPS + 1,)), dma((SWEEPS + 1,)),
                dma((SWEEPS, 15)), dma((SWEEPS, 15)),
            ],
            compiler_params=pltpu.CompilerParams(
                collective_id=0, has_side_effects=True, vmem_limit_bytes=56 * 1024 * 1024
            ),
        )(x_blk, b_own, c_full, ridge_lam.reshape(1, 1))

    return jax.shard_map(
        local_sweeps,
        mesh=mesh,
        in_specs=(P("tube", "row", "col"), P(("col", "row", "tube"), None), P(None, None), P()),
        out_specs=(P(("row", "col", "tube"), None), P(("col", "row", "tube"), None), P(None, None)),
        check_vma=False,
    )
```

time: 605 us -> 113 us (0.19); the launches traced: 596 us -> 112 us
  waiting for transfers between devices: 241 us -> 0 us
  other arithmetic: 151 us -> 0 us
  Pallas kernels: 0 us -> 107 us
  blocking collectives: 105 us -> 0 us
  matrix products: 75.2 us -> 0 us
  between operations: 17.2 us -> 1.29 us
    psum x5 -> x0, waiting for transfers between devices: 228 us -> none  [the longest x3 128 us: local_sweeps(): gram_b = lax.psum(gram_of(b_own), ALL_AXES)]
    another operation x30 -> x0, other arithmetic: 137 us -> none  [the longest x18 74.3 us: solve_rows(): chol_fac = jnp.linalg.cholesky(gram_prod + ridge_lam * ident_mat)]
    pallas_call x0 -> x1, Pallas kernels: none -> 107 us  [local_sweeps(): pl.pallas_call(kernel, name='als', out_shape=(jax.ShapeDtypeStruct((arows...]
    all_gather x7 -> x0, blocking collectives: 77 us -> none  [the longest x3 52.6 us: local_sweeps(): b_cols = lax.all_gather(b_own, ('row', 'tube'), axis=0, tiled=True)]
    dot_general x15 -> x0, matrix products: 68.2 us -> none  [the longest x2 25.2 us: local_sweeps(): jnp.einsum('kjr,kr->jr', v_kjr, c_blk, preferred_element_type=jnp.float32...]
    psum x2 -> x0, blocking collectives: 27.5 us -> none  [local_sweeps(): c_local = lax.psum(part_c, ('row', 'col'))]
    reduce_scatter x2 -> x0, waiting for transfers between devices: 12.7 us -> none  [local_sweeps(): lax.psum_scatter(part_b, ('row', 'tube'), scatter_dimension=0, tiled=True)]
    convert_element_type x1 -> x0, other arithmetic: 9.11 us -> none  [local_sweeps(): x_half = x_blk.astype(jnp.bfloat16)]
  transfers between devices with their start and end apart: 9 -> 0, of which waited for: 7 -> 0; matrix products, arithmetic and copies ran while one was open for 24% -> 0% of each run, Pallas kernels for 0% -> 0%
where the time goes in v1:
time: 113 us; the launch traced here: 112 us
  Pallas kernels  107 us (95%)
  local copies, waits for them, and re-layouts  4.17 us (4%)
  between operations  1.29 us (1%)
    pallas_call x1, Pallas kernels, local_sweeps(): pl.pallas_call(kernel, name='als', out_shape=(jax.ShapeDtypeStruct((arows...  107 us
    unnamed x3, local copies, waits for them, and re-layouts  4.17 us

profile of v1, /device:TPU:0, one launch (start us, length us, event | category | flops | bytes accessed | tf_op | source)
XLA Modules:
  0.0 112.3 jit_solution(4320853705475592636)
XLA Ops:
  1.3 106.8 %als.1 = (f32[64,128]{1,0:T(8,128)}, f32[128,128]{1,0:T(8,128)}, f32[32,128]{1,0:T(8,128)}) custom-call(f32[16,256,1024]{2,1,0:T(8,128)} %x_hbm.1, f32[128,128]{1,0:T(8,128)} %b_ref.1, f32[32,128]{1,0:T(8,128)} %c_ref.1, f32[1,1]{1,0:T(1,128)} %bitcast.1.lam_ref), custom_call_target="tpu_custom_call" | custom-call | tf_op jit(solution)/shard_map/als/pallas_call | solution.py:249
  108.1 1.4 %copy.11 = f32[64,128]{1,0:T(8,128)} copy(f32[64,128]{1,0:T(8,128)} %get-tuple-element.6) | data formatting | bytes 65536
  109.5 1.5 %copy.12 = f32[128,128]{1,0:T(8,128)} copy(f32[128,128]{1,0:T(8,128)} %get-tuple-element.7) | data formatting | bytes 131072
  111.0 1.3 %copy.13 = f32[32,128]{1,0:T(8,128)} copy(f32[32,128]{1,0:T(8,128)} %get-tuple-element.8) | data formatting | bytes 32768

commit v2 on v1

--- a/solution.py
+++ b/solution.py
@@ -25,7 +25,7 @@
     x_hbm, b_ref, c_ref, lam_ref,
     a_out, b_out, c_out,
     xf, xh, u_ref, bcols, a16, at_ref, af, pa, rsa, vt, rsb, gbp, gbr, pc, cb,
-    w_ref, q_ref, li_ref, inv_ref, ga_ref, gb_ref, cfac,
+    w_ref, e_ref, li_ref, inv_ref, ga_ref, gb_ref, cfac,
     x_sem, rsa_s, rsa_r, aga_s, aga_r, af_s, af_r, rsb_s, rsb_r, agb_s, agb_r, gb_s, gb_r, pc_s, pc_r,
 ):
     t = lax.axis_index("tube")
@@ -86,37 +86,58 @@
         eye = jnp.where(rows == cols, 1.0, 0.0).astype(F32)
         w_ref[:, :rank] = gram_prod + lam_ref[0, 0] * eye
         w_ref[:, rank:] = eye
-        q_ref[...] = jnp.zeros_like(q_ref)
         r1 = lax.broadcasted_iota(jnp.int32, (8, rank), 0)
-        r2 = lax.broadcasted_iota(jnp.int32, (8, 2 * rank), 0)
-
-        def body(b, _):
-            off = pl.multiple_of(b * 8, 8)
-            pan = w_ref[pl.ds(off, 8), :]
-            rolled = pltpu.roll(pan[:, :rank], rank - off, axis=1)
-            e = [jnp.broadcast_to(rolled[:, n : n + 1], (8, rank)) for n in range(8)]
-            chol = jnp.zeros_like(pan)
+
+        def lane(x, n):
+            return jnp.take_along_axis(x, jnp.full((8, rank), n, jnp.int32), axis=1, mode="promise_in_bounds")
+
+        def step(b, first):
+            lo = pl.multiple_of(b * 8, 8)
+            ps = w_ref[pl.ds(lo, 8), :rank]
+            pi = w_ref[pl.ds(lo, 8), rank:]
+            e = [lane(ps, lo + n) for n in range(8)]
+            for n in range(8):
+                for v in range(first, rank // 8):
+                    e_ref[v, n] = lane(w_ref[8 * v : 8 * v + 8, :rank], lo + n)
+            low = None
+            piv = jnp.broadcast_to(e[0][0:1], (8, rank))
             for j in range(8):
-                piv = jnp.broadcast_to(e[j][j : j + 1], (8, rank))
                 isq = lax.rsqrt(piv)
                 rc = isq * isq
+                if j < 7:
+                    x = jnp.broadcast_to(e[j + 1][j : j + 1], (8, rank))
+                    piv = jnp.broadcast_to(e[j + 1][j + 1 : j + 2], (8, rank)) - (x * x) * rc
                 m = e[j] * rc
-                m2 = jnp.concatenate([m, m], axis=1)
-                isq2 = jnp.concatenate([isq, isq], axis=1)
-                rc2 = jnp.concatenate([rc, rc], axis=1)
-                pj = jnp.broadcast_to(pan[j : j + 1], (8, 2 * rank))
-                chol = jnp.where(r2 == j, pj * isq2, chol)
-                pan = jnp.where(r2 == j, pj * rc2, pan - m2 * pj)
+                hit = r1 == j
+                pjs = jnp.broadcast_to(ps[j : j + 1], (8, rank))
+                pji = jnp.broadcast_to(pi[j : j + 1], (8, rank))
+                low = pji * isq if low is None else jnp.where(hit, pji * isq, low)
+                ps = jnp.where(hit, pjs * rc, ps - m * pjs)
+                pi = jnp.where(hit, pji * rc, pi - m * pji)
                 for n in range(j + 1, 8):
                     en = jnp.broadcast_to(e[n][j : j + 1], (8, rank))
-                    e[n] = jnp.where(r1 == j, en * rc, e[n] - m * en)
-            li_ref[pl.ds(off, 8), :] = chol[:, rank:]
-            q_ref[pl.ds(off, 8), :] = pan
-            w_ref[...] = w_ref[...] - jnp.dot(w_ref[:, :rank], q_ref[...], precision=HI, preferred_element_type=F32)
-            q_ref[pl.ds(off, 8), :] = jnp.zeros_like(pan)
-            return 0
-
-        lax.fori_loop(0, rank // 8, body, 0)
+                    e[n] = jnp.where(hit, en * rc, e[n] - m * en)
+            li_ref[pl.ds(lo, 8), :] = low
+            qs = [jnp.broadcast_to(ps[n : n + 1], (8, rank)) for n in range(8)]
+            qi = [jnp.broadcast_to(pi[n : n + 1], (8, rank)) for n in range(8)]
+            for v in range(first, rank // 8):
+                ds = [e_ref[v, n] * qs[n] for n in range(8)]
+                di = [e_ref[v, n] * qi[n] for n in range(8)]
+                while len(ds) > 1:
+                    ds = [ds[n] + ds[n + 1] for n in range(0, len(ds), 2)]
+                    di = [di[n] + di[n + 1] for n in range(0, len(di), 2)]
+                w_ref[8 * v : 8 * v + 8, :rank] -= ds[0]
+                w_ref[8 * v : 8 * v + 8, rank:] -= di[0]
+
+        def run(lo, hi):
+            def body(b, _):
+                step(b, lo)
+                return 0
+
+            lax.fori_loop(lo, hi, body, 0)
+
+        run(0, 8)
+        run(8, 16)
         inv_ref[...] = dot_t0(li_ref[...], li_ref[...], precision=HI)
 
     bcols[0, q] = b_ref[...].astype(BF16)
@@ -275,7 +296,7 @@
                 pltpu.VMEM((SWEEPS, 16, kk, rank), F32),
                 pltpu.VMEM((kk, rank, rank), F32),
                 pltpu.VMEM((rank, 2 * rank), F32),
-                pltpu.VMEM((rank, 2 * rank), F32),
+                pltpu.VMEM((rank // 8, 8, 8, rank), F32),
                 pltpu.VMEM((rank, rank), F32),
                 pltpu.VMEM((rank, rank), F32),
                 pltpu.VMEM((rank, rank), F32),

time: 113 us -> 92 us (0.81)
  Pallas kernels: 107 us -> 86.2 us
    pallas_call x1, Pallas kernels: 107 us -> 86.2 us  [local_sweeps(): pl.pallas_call(kernel, name='als', out_shape=(jax.ShapeDtypeStruct((arows...]
where the time goes in v2:
time: 92 us; the launch traced here: 91.7 us
  Pallas kernels  86.2 us (94%)
  local copies, waits for them, and re-layouts  4.17 us (5%)
  between operations  1.29 us (1%)
    pallas_call x1, Pallas kernels, local_sweeps(): pl.pallas_call(kernel, name='als', out_shape=(jax.ShapeDtypeStruct((arows...  86.2 us
    unnamed x3, local copies, waits for them, and re-layouts  4.17 us

profile of v2, /device:TPU:0, one launch (start us, length us, event | category | flops | bytes accessed | tf_op | source)
XLA Modules:
  0.0 91.7 jit_solution(1424802803151212207)
XLA Ops:
  1.3 86.2 %als.1 = (f32[64,128]{1,0:T(8,128)}, f32[128,128]{1,0:T(8,128)}, f32[32,128]{1,0:T(8,128)}) custom-call(f32[16,256,1024]{2,1,0:T(8,128)} %x_hbm.1, f32[128,128]{1,0:T(8,128)} %b_ref.1, f32[32,128]{1,0:T(8,128)} %c_ref.1, f32[1,1]{1,0:T(1,128)} %bitcast.1.lam_ref), custom_call_target="tpu_custom_call" | custom-call | tf_op jit(solution)/shard_map/als/pallas_call | solution.py:270
  87.5 1.4 %copy.11 = f32[64,128]{1,0:T(8,128)} copy(f32[64,128]{1,0:T(8,128)} %get-tuple-element.6) | data formatting | bytes 65536
  88.9 1.5 %copy.12 = f32[128,128]{1,0:T(8,128)} copy(f32[128,128]{1,0:T(8,128)} %get-tuple-element.7) | data formatting | bytes 131072
  90.4 1.3 %copy.13 = f32[32,128]{1,0:T(8,128)} copy(f32[32,128]{1,0:T(8,128)} %get-tuple-element.8) | data formatting | bytes 32768

commit v3 on v2

--- a/solution.py
+++ b/solution.py
@@ -11,10 +11,10 @@
 F32 = jnp.float32
 BF16 = jnp.bfloat16
 
-OFF_YZ = [(t, c, 0) for c in range(2) for t in range(2)][1:]
-OFF_XZ = [(t, 0, w) for w in range(4) for t in range(2)][1:]
-OFF_ALL_REST = [(t, c, w) for w in range(1, 4) for c in range(2) for t in range(2)]
-OFF_ALL = OFF_YZ + OFF_ALL_REST
+YZ = [(1, 1, 0, 0), (0, 1, 0, 0), (1, 0, 0, 0)]
+NEAR = [(1, 0, 0, 1), (1, 0, 0, 0), (0, 0, 0, 1)]
+FAR = [(1, 0, 1, 1), (1, 0, 1, 0), (0, 0, 1, 1), (0, 0, 1, 0)]
+ALL = YZ + [(t, c, x, k) for x, k in ((1, 1), (1, 0), (0, 1)) for c in (1, 0) for t in (1, 0)]
 
 
 def dot_t0(a, b, **kw):
@@ -22,31 +22,54 @@
 
 
 def kernel(
-    x_hbm, b_ref, c_ref, lam_ref,
-    a_out, b_out, c_out,
-    xf, xh, u_ref, bcols, a16, at_ref, af, pa, rsa, vt, rsb, gbp, gbr, pc, cb,
+    x_hbm, b_hbm, c_hbm, lam_ref,
+    out,
+    xf, xh, u_ref, b_in, bcols, a16, at_ref, af, pa, rsa, vp, vpr, vo, rsb, gbp, gbr, pc, cb,
     w_ref, e_ref, li_ref, inv_ref, ga_ref, gb_ref, cfac,
-    x_sem, rsa_s, rsa_r, aga_s, aga_r, af_s, af_r, rsb_s, rsb_r, agb_s, agb_r, gb_s, gb_r, pc_s, pc_r,
+    x_sem, in_sem, rsa_s, rsa_r, aga_s, aga_r, af_s, af_r, vp_s, vp_r, rsb_s, rsb_r, agb_s, agb_r, gb_s, gb_r, pc_s, pc_r,
 ):
     t = lax.axis_index("tube")
     c = lax.axis_index("col")
     w = lax.axis_index("row")
+    xc, core = w // 2, w % 2
     kk, ii, jj = xf.shape
-    rank = b_ref.shape[1]
+    rank = b_in.shape[1]
     g = c * 2 + t
-    q = w * 2 + t
     me = g * 4 + w
 
-    for k in range(kk):
+    ins = [
+        pltpu.make_async_copy(b_hbm, b_in, in_sem.at[0]),
+        pltpu.make_async_copy(c_hbm, cfac, in_sem.at[1]),
+    ]
+    for cp in ins:
+        cp.start()
+    depth = 4
+    for k in range(depth):
         pltpu.make_async_copy(x_hbm.at[k], xf.at[k], x_sem.at[k]).start()
 
+    def load(k, _):
+        pltpu.make_async_copy(x_hbm.at[k], xf.at[k], x_sem.at[k]).wait()
+
+        @pl.when(k + depth < kk)
+        def _():
+            pltpu.make_async_copy(x_hbm.at[k + depth], xf.at[k + depth], x_sem.at[k + depth]).start()
+
+        for n in range(jj // ii):
+            xh[k, n] = xf[k, :, n * ii : (n + 1) * ii].astype(BF16)
+        return 0
+
     def dev(off):
-        return ((t + off[0]) % 2, (c + off[1]) % 2, (w + off[2]) % 4)
+        return ((t + off[0]) % 2, (c + off[1]) % 2, ((xc + off[2]) % 2) * 2 + (core + off[3]) % 2)
 
     barrier = pltpu.get_barrier_semaphore()
-    for off in OFF_ALL:
+    for off in reversed(ALL):
         pl.semaphore_signal(barrier, inc=1, device_id=dev(off), device_id_type=MESH)
-    pl.semaphore_wait(barrier, len(OFF_ALL))
+    for cp in ins:
+        cp.wait()
+    bcols[0, w, t] = b_in[...].astype(BF16)
+    first = 4
+    lax.fori_loop(0, first, load, 0)
+    pl.semaphore_wait(barrier, len(ALL))
 
     def push(src, dst, ss, rs, off):
         return pltpu.make_async_remote_copy(
@@ -55,26 +78,36 @@
 
     def gather_b(s):
         return [
-            push(bcols.at[s, q], bcols.at[s, q], agb_s.at[s, n], agb_r.at[s, n], off)
-            for n, off in enumerate(OFF_XZ)
+            push(bcols.at[s, w, t], bcols.at[s, w, t], agb_s.at[s, n], agb_r.at[s, n], off)
+            for n, off in enumerate(NEAR + FAR)
         ]
 
     def gram_copy(s):
-        return push(gbp, gbr.at[s], gb_s.at[s], gb_r.at[s], (0, 1, 0))
-
-    def u_pass(s):
-        bmat = bcols[s].reshape(jj, rank)
-
+        return push(gbp, gbr.at[s], gb_s.at[s], gb_r.at[s], (0, 1, 0, 0))
+
+    def half_u(s, x2, first):
         def body(k, _):
-            u_ref[k] = jnp.dot(xh[k], bmat, preferred_element_type=F32)
+            acc = None if first else u_ref[k]
+            for n in range(2):
+                p = jnp.dot(
+                    xh[k, x2 * 2 + n], bcols[s, x2 * 2 + n].reshape(2 * rank, rank), preferred_element_type=F32
+                )
+                acc = p if acc is None else acc + p
+            u_ref[k] = acc
             return 0
 
-        lax.fori_loop(0, kk, body, 0)
-
-    def start_gram_b(s):
+        lax.fori_loop(0, kk, body, 0, unroll=8)
+
+    def gather_and_u(s, cps):
+        for cp in cps[:3]:
+            cp.wait()
+        half_u(s, xc, True)
+        for cp in cps[3:]:
+            cp.wait()
         bmat = bcols[s].reshape(jj, rank)
         gbp[...] = dot_t0(bmat, bmat)
         gram_copy(s).start()
+        half_u(s, 1 - xc, False)
 
     def finish_gram_b(s):
         gram_copy(s).wait()
@@ -140,22 +173,12 @@
         run(8, 16)
         inv_ref[...] = dot_t0(li_ref[...], li_ref[...], precision=HI)
 
-    bcols[0, q] = b_ref[...].astype(BF16)
     cps = gather_b(0)
     for cp in cps:
         cp.start()
-    cfac[...] = c_ref[...]
-
-    def load(k, _):
-        pltpu.make_async_copy(x_hbm.at[k], xf.at[k], x_sem.at[k]).wait()
-        xh[k] = xf[k].astype(BF16)
-        return 0
-
-    lax.fori_loop(0, kk, load, 0)
-    for cp in cps:
-        cp.wait()
-    start_gram_b(0)
-    u_pass(0)
+
+    lax.fori_loop(first, kk, load, 0)
+    gather_and_u(0, cps)
     finish_gram_b(0)
 
     def sweep(s, _):
@@ -168,7 +191,7 @@
         part = lax.fori_loop(0, kk, body_a, jnp.zeros((ii, rank), F32))
         pa[...] = part.reshape(pa.shape)
         ra = []
-        for n, off in enumerate(OFF_YZ):
+        for n, off in enumerate(YZ):
             g2 = dev(off)[1] * 2 + dev(off)[0]
             ra.append(push(pa.at[g2], rsa.at[s, n], rsa_s.at[s, n], rsa_r.at[s, n], off))
         for cp in ra:
@@ -178,15 +201,15 @@
             cp.wait()
         mtt_a = pa[g] + rsa[s, 0] + rsa[s, 1] + rsa[s, 2]
         a_own = jnp.dot(mtt_a, inv_ref[...], precision=HI, preferred_element_type=F32)
-        a_out[...] = a_own
         a16[s, w, g] = a_own.astype(BF16)
         af[s, g] = a_own
-        ga = [push(a16.at[s, w, g], a16.at[s, w, g], aga_s.at[s, n], aga_r.at[s, n], off) for n, off in enumerate(OFF_ALL)]
+        ga = [push(a16.at[s, w, g], a16.at[s, w, g], aga_s.at[s, n], aga_r.at[s, n], off) for n, off in enumerate(ALL)]
         for cp in ga:
             cp.start()
-        fa = [push(af.at[s, g], af.at[s, g], af_s.at[s, n], af_r.at[s, n], off) for n, off in enumerate(OFF_YZ)]
+        fa = [push(af.at[s, g], af.at[s, g], af_s.at[s, n], af_r.at[s, n], off) for n, off in enumerate(YZ)]
         for cp in fa:
             cp.start()
+        out[: a_own.shape[0], :] = a_own
 
         cmine = cfac[pl.ds(pl.multiple_of(t * kk, kk), kk), :]
         ct = jnp.transpose(jnp.concatenate([cmine, jnp.zeros((rank - kk, rank), F32)], axis=0))
@@ -195,22 +218,30 @@
         for cp in ga[:3]:
             cp.wait()
         at_ref[...] = jnp.transpose(a16[s, w].reshape(ii, rank))
-        vt[...] = jnp.zeros_like(vt)
-
-        def body_b(k, _):
-            v = jnp.dot(at_ref[...], xh[k], preferred_element_type=F32)
-            ck = cb[k]
-            for n in range(jj // rank):
-                vt[n] += v[:, n * rank : (n + 1) * rank] * ck
-            return 0
-
-        lax.fori_loop(0, kk, body_b, 0)
+
+        def chunk(wc):
+            def body(k, acc):
+                ck = cb[k]
+                return acc + jnp.dot(at_ref[...], xh[k, wc], preferred_element_type=F32) * jnp.concatenate([ck, ck], axis=1)
+
+            return lax.fori_loop(0, kk, body, jnp.zeros((rank, ii), F32), unroll=16)
+
+        vc = []
+        for n in range(2):
+            vp[n] = chunk(((xc + 1 - n) % 2) * 2 + (1 - core))
+            vc.append(push(vp.at[n], vpr.at[s, n], vp_s.at[s, n], vp_r.at[s, n], (0, 0, 0, 1)))
+            vc[n].start()
         rb = []
-        for n, off in enumerate(OFF_XZ):
-            q2 = dev(off)[2] * 2 + dev(off)[0]
-            rb.append(push(vt.at[q2], rsb.at[s, n], rsb_s.at[s, n], rsb_r.at[s, n], off))
-        for cp in rb:
-            cp.start()
+        for n in range(2):
+            mine = chunk(((xc + 1 - n) % 2) * 2 + core)
+            vc[n].wait()
+            mine = mine + vpr[s, n]
+            vo[n, 0] = mine[:, :rank]
+            vo[n, 1] = mine[:, rank:]
+            for off in ((1, 0, 1, 0), (0, 0, 1, 0)) if n == 0 else ((1, 0, 0, 0),):
+                m = len(rb)
+                rb.append(push(vo.at[n, dev(off)[0]], rsb.at[s, m], rsb_s.at[s, m], rsb_r.at[s, m], off))
+                rb[m].start()
         for cp in ga[3:]:
             cp.wait()
         aall = a16[s].reshape(4 * ii, rank)
@@ -218,27 +249,22 @@
         factor(ga_ref[...] * gram_c)
         for cp in rb:
             cp.wait()
-        mtt_b = vt[q]
-        for n in range(len(OFF_XZ)):
-            mtt_b = mtt_b + rsb[s, n]
+        mtt_b = vo[1, t] + rsb[s, 0] + rsb[s, 1] + rsb[s, 2]
         b_own = jnp.transpose(jnp.dot(inv_ref[...], mtt_b, precision=HI, preferred_element_type=F32))
-        b_out[...] = b_own
-        bcols[s + 1, q] = b_own.astype(BF16)
+        bcols[s + 1, w, t] = b_own.astype(BF16)
         gcs = gather_b(s + 1)
         for cp in gcs:
             cp.start()
-        for cp in gcs:
-            cp.wait()
-
-        start_gram_b(s + 1)
-        u_pass(s + 1)
+        out[ii // 4 : ii // 4 + rank, :] = b_own
+
+        gather_and_u(s + 1, gcs)
         for cp in fa:
             cp.wait()
         afull = af[s].reshape(ii, rank)
         pc[s, me] = jnp.concatenate(
             [jnp.sum(u_ref[k] * afull, axis=0, keepdims=True) for k in range(kk)], axis=0
         )
-        cs = [push(pc.at[s, me], pc.at[s, me], pc_s.at[s, n], pc_r.at[s, n], off) for n, off in enumerate(OFF_ALL)]
+        cs = [push(pc.at[s, me], pc.at[s, me], pc_s.at[s, n], pc_r.at[s, n], off) for n, off in enumerate(ALL)]
         for cp in cs:
             cp.start()
         finish_gram_b(s + 1)
@@ -257,40 +283,60 @@
         return 0
 
     lax.fori_loop(0, SWEEPS, sweep, 0)
-    c_out[...] = cfac[...]
+    out[ii // 4 + rank :, :] = cfac[...]
+
+
+def split(rows, packed):
+    def copy(src, *dsts):
+        at = 0
+        for n, dst in zip(rows, dsts):
+            dst[...] = src[at : at + n, :]
+            at += n
+
+    vmem = pl.BlockSpec(memory_space=pltpu.VMEM)
+    return pl.pallas_call(
+        copy,
+        name="results",
+        out_shape=tuple(jax.ShapeDtypeStruct((n, packed.shape[1]), packed.dtype) for n in rows),
+        in_specs=[vmem],
+        out_specs=(vmem,) * len(rows),
+        compiler_params=pltpu.CompilerParams(vmem_limit_bytes=1024 * 1024),
+    )(packed)
 
 
 def solution(mesh):
     def local_sweeps(x_blk, b_own, c_full, ridge_lam):
         kk, ii, jj = x_blk.shape
-        rank = b_own.shape[1]
-        arows, brows = ii // 4, b_own.shape[0]
+        brows, rank = b_own.shape
+        arows, crows = ii // 4, c_full.shape[0]
         dma = pltpu.SemaphoreType.DMA
         vmem = pl.BlockSpec(memory_space=pltpu.VMEM)
-        return pl.pallas_call(
+        hbm = pl.BlockSpec(memory_space=pl.ANY)
+
+        def sems(*shape):
+            return [dma(shape), dma(shape)]
+
+        packed = pl.pallas_call(
             kernel,
             name="als",
-            out_shape=(
-                jax.ShapeDtypeStruct((arows, rank), F32),
-                jax.ShapeDtypeStruct((brows, rank), F32),
-                jax.ShapeDtypeStruct(c_full.shape, F32),
-            ),
-            in_specs=[
-                pl.BlockSpec(memory_space=pl.ANY), vmem, vmem, pl.BlockSpec(memory_space=pltpu.SMEM),
-            ],
-            out_specs=(vmem, vmem, vmem),
+            out_shape=jax.ShapeDtypeStruct((arows + brows + crows, rank), F32),
+            in_specs=[hbm, hbm, hbm, pl.BlockSpec(memory_space=pltpu.SMEM)],
+            out_specs=vmem,
             scratch_shapes=[
                 pltpu.VMEM((kk, ii, jj), F32),
-                pltpu.VMEM((kk, ii, jj), BF16),
+                pltpu.VMEM((kk, jj // ii, ii, ii), BF16),
                 pltpu.VMEM((kk, ii, rank), F32),
-                pltpu.VMEM((SWEEPS + 1, 8, brows, rank), BF16),
+                pltpu.VMEM((brows, rank), F32),
+                pltpu.VMEM((SWEEPS + 1, 4, 2, brows, rank), BF16),
                 pltpu.VMEM((SWEEPS, 4, 4, arows, rank), BF16),
                 pltpu.VMEM((rank, ii), BF16),
                 pltpu.VMEM((SWEEPS, 4, arows, rank), F32),
                 pltpu.VMEM((4, arows, rank), F32),
                 pltpu.VMEM((SWEEPS, 3, arows, rank), F32),
-                pltpu.VMEM((8, rank, brows), F32),
-                pltpu.VMEM((SWEEPS, 7, rank, brows), F32),
+                pltpu.VMEM((2, rank, 2 * brows), F32),
+                pltpu.VMEM((SWEEPS, 2, rank, 2 * brows), F32),
+                pltpu.VMEM((2, 2, rank, brows), F32),
+                pltpu.VMEM((SWEEPS, 3, rank, brows), F32),
                 pltpu.VMEM((rank, rank), F32),
                 pltpu.VMEM((SWEEPS + 1, rank, rank), F32),
                 pltpu.VMEM((SWEEPS, 16, kk, rank), F32),
@@ -302,19 +348,15 @@
                 pltpu.VMEM((rank, rank), F32),
                 pltpu.VMEM((rank, rank), F32),
                 pltpu.VMEM(c_full.shape, F32),
-                dma((kk,)),
-                dma((SWEEPS, 3)), dma((SWEEPS, 3)),
-                dma((SWEEPS, 15)), dma((SWEEPS, 15)),
-                dma((SWEEPS, 3)), dma((SWEEPS, 3)),
-                dma((SWEEPS, 7)), dma((SWEEPS, 7)),
-                dma((SWEEPS + 1, 7)), dma((SWEEPS + 1, 7)),
-                dma((SWEEPS + 1,)), dma((SWEEPS + 1,)),
-                dma((SWEEPS, 15)), dma((SWEEPS, 15)),
+                dma((kk,)), dma((2,)),
+                *sems(SWEEPS, 3), *sems(SWEEPS, 15), *sems(SWEEPS, 3), *sems(SWEEPS, 2), *sems(SWEEPS, 3),
+                *sems(SWEEPS + 1, 7), *sems(SWEEPS + 1), *sems(SWEEPS, 15),
             ],
             compiler_params=pltpu.CompilerParams(
                 collective_id=0, has_side_effects=True, vmem_limit_bytes=56 * 1024 * 1024
             ),
         )(x_blk, b_own, c_full, ridge_lam.reshape(1, 1))
+        return split((arows, brows, crows), packed)
 
     return jax.shard_map(
         local_sweeps,

time: 92 us -> 81.7 us (0.89)
  Pallas kernels: 86.2 us -> 79.4 us
  local copies, waits for them, and re-layouts: 4.17 us -> 0.89 us
    pallas_call x1 -> x2, Pallas kernels: 86.2 us -> 79.4 us  [the longest x1 78.7 us: local_sweeps(): pl.pallas_call(kernel, name='als', out_shape=jax.ShapeDtypeStruct((arows...]
    unnamed x3 -> x2, local copies, waits for them, and re-layouts: 4.17 us -> 0.89 us
where the time goes in v3:
time: 81.7 us; the launch traced here: 81.6 us
  Pallas kernels  79.4 us (97%)
  between operations  1.29 us (2%)
  local copies, waits for them, and re-layouts  0.89 us (1%)
    pallas_call x1, Pallas kernels, local_sweeps(): pl.pallas_call(kernel, name='als', out_shape=jax.ShapeDtypeStruct((arows...  78.7 us

profile of v3, /device:TPU:0, one launch (start us, length us, event | category | flops | bytes accessed | tf_op | source)
XLA Modules:
  0.0 81.6 jit_solution(5468804609243594035)
XLA Ops:
  1.3 78.7 %als.1.src = f32[224,128]{1,0:T(8,128)} custom-call(f32[16,256,1024]{2,1,0:T(8,128)} %x_hbm.1, f32[128,128]{1,0:T(8,128)} %b_hbm.1, f32[32,128]{1,0:T(8,128)} %c_hbm.1, f32[1,1]{1,0:T(1,128)} %bitcast.1.lam_ref), custom_call_target="tpu_custom_call" | custom-call | tf_op jit(solution)/shard_map/als/pallas_call | solution.py:319
  80.0 0.0 copy-start
  80.0 0.9 %copy-done = f32[224,128]{1,0:T(8,128)S(1)} copy-done((f32[224,128]{1,0:T(8,128)S(1)}, f32[224,128]{1,0:T(8,128)}, u32[]{:S(2)}) %copy-start) | copy-done | bytes 114712
  80.9 0.6 results.1
Async XLA Ops:
  80.0 0.9 %copy-start = (f32[224,128]{1,0:T(8,128)S(1)}, f32[224,128]{1,0:T(8,128)}, u32[]{:S(2)}) copy-start(f32[224,128]{1,0:T(8,128)} %als.1.src) | copy-start | bytes 344068

commit v4 on v3

--- a/solution.py
+++ b/solution.py
@@ -12,8 +12,8 @@
 BF16 = jnp.bfloat16
 
 YZ = [(1, 1, 0, 0), (0, 1, 0, 0), (1, 0, 0, 0)]
-NEAR = [(1, 0, 0, 1), (1, 0, 0, 0), (0, 0, 0, 1)]
-FAR = [(1, 0, 1, 1), (1, 0, 1, 0), (0, 0, 1, 1), (0, 0, 1, 0)]
+SAME_CORE = [(1, 0, 1, 0), (0, 0, 1, 0), (1, 0, 0, 0)]
+PARTNER = (0, 0, 0, 1)
 ALL = YZ + [(t, c, x, k) for x, k in ((1, 1), (1, 0), (0, 1)) for c in (1, 0) for t in (1, 0)]
 
 
@@ -76,38 +76,44 @@
             src_ref=src, dst_ref=dst, send_sem=ss, recv_sem=rs, device_id=dev(off), device_id_type=MESH
         )
 
+    def b_copy(s, n, src, off):
+        block = bcols.at[s, src[2], src[0]]
+        return push(block, block, agb_s.at[s, n], agb_r.at[s, n], off)
+
     def gather_b(s):
-        return [
-            push(bcols.at[s, w, t], bcols.at[s, w, t], agb_s.at[s, n], agb_r.at[s, n], off)
-            for n, off in enumerate(NEAR + FAR)
-        ]
+        cps = [b_copy(s, n, (t, c, w), off) for n, off in enumerate(SAME_CORE + [PARTNER])]
+        for cp in cps:
+            cp.start()
+        return cps
+
+    def relay_b(s, cps):
+        fwd = []
+        for n, off in reversed(list(enumerate(SAME_CORE))):
+            cps[n].wait()
+            fwd.append(b_copy(s, 4 + n, dev(off), PARTNER))
+            fwd[-1].start()
+        cps[3].wait()
+        for cp in fwd:
+            cp.wait()
 
     def gram_copy(s):
         return push(gbp, gbr.at[s], gb_s.at[s], gb_r.at[s], (0, 1, 0, 0))
 
-    def half_u(s, x2, first):
+    def gather_and_u(s, cps):
+        relay_b(s, cps)
+        bmat = bcols[s].reshape(jj, rank)
+        gbp[...] = dot_t0(bmat, bmat)
+        gram_copy(s).start()
+
         def body(k, _):
-            acc = None if first else u_ref[k]
-            for n in range(2):
-                p = jnp.dot(
-                    xh[k, x2 * 2 + n], bcols[s, x2 * 2 + n].reshape(2 * rank, rank), preferred_element_type=F32
-                )
+            acc = None
+            for n in range(4):
+                p = jnp.dot(xh[k, n], bcols[s, n].reshape(2 * rank, rank), preferred_element_type=F32)
                 acc = p if acc is None else acc + p
             u_ref[k] = acc
             return 0
 
-        lax.fori_loop(0, kk, body, 0, unroll=8)
-
-    def gather_and_u(s, cps):
-        for cp in cps[:3]:
-            cp.wait()
-        half_u(s, xc, True)
-        for cp in cps[3:]:
-            cp.wait()
-        bmat = bcols[s].reshape(jj, rank)
-        gbp[...] = dot_t0(bmat, bmat)
-        gram_copy(s).start()
-        half_u(s, 1 - xc, False)
+        lax.fori_loop(0, kk, body, 0, unroll=4)
 
     def finish_gram_b(s):
         gram_copy(s).wait()
@@ -124,36 +130,41 @@
         def lane(x, n):
             return jnp.take_along_axis(x, jnp.full((8, rank), n, jnp.int32), axis=1, mode="promise_in_bounds")
 
-        def step(b, first):
+        def spread(x, n):
+            return jnp.broadcast_to(x[n : n + 1], (8, rank))
+
+        def step(b, first, last):
             lo = pl.multiple_of(b * 8, 8)
             ps = w_ref[pl.ds(lo, 8), :rank]
             pi = w_ref[pl.ds(lo, 8), rank:]
             e = [lane(ps, lo + n) for n in range(8)]
             for n in range(8):
-                for v in range(first, rank // 8):
+                for v in range(first, last):
                     e_ref[v, n] = lane(w_ref[8 * v : 8 * v + 8, :rank], lo + n)
-            low = None
-            piv = jnp.broadcast_to(e[0][0:1], (8, rank))
+            low_s = low_i = None
+            piv = spread(e[0], 0)
             for j in range(8):
                 isq = lax.rsqrt(piv)
                 rc = isq * isq
                 if j < 7:
-                    x = jnp.broadcast_to(e[j + 1][j : j + 1], (8, rank))
-                    piv = jnp.broadcast_to(e[j + 1][j + 1 : j + 2], (8, rank)) - (x * x) * rc
+                    x = spread(e[j + 1], j)
+                    piv = spread(e[j + 1], j + 1) - (x * x) * rc
                 m = e[j] * rc
                 hit = r1 == j
-                pjs = jnp.broadcast_to(ps[j : j + 1], (8, rank))
-                pji = jnp.broadcast_to(pi[j : j + 1], (8, rank))
-                low = pji * isq if low is None else jnp.where(hit, pji * isq, low)
+                pjs = spread(ps, j)
+                pji = spread(pi, j)
+                low_s = pjs * isq if low_s is None else jnp.where(hit, pjs * isq, low_s)
+                low_i = pji * isq if low_i is None else jnp.where(hit, pji * isq, low_i)
                 ps = jnp.where(hit, pjs * rc, ps - m * pjs)
                 pi = jnp.where(hit, pji * rc, pi - m * pji)
                 for n in range(j + 1, 8):
-                    en = jnp.broadcast_to(e[n][j : j + 1], (8, rank))
+                    en = spread(e[n], j)
                     e[n] = jnp.where(hit, en * rc, e[n] - m * en)
-            li_ref[pl.ds(lo, 8), :] = low
-            qs = [jnp.broadcast_to(ps[n : n + 1], (8, rank)) for n in range(8)]
-            qi = [jnp.broadcast_to(pi[n : n + 1], (8, rank)) for n in range(8)]
-            for v in range(first, rank // 8):
+            li_ref[pl.ds(lo, 8), :rank] = low_s
+            li_ref[pl.ds(lo, 8), rank:] = low_i
+            qs = [spread(ps, n) for n in range(8)]
+            qi = [spread(pi, n) for n in range(8)]
+            for v in range(first, last):
                 ds = [e_ref[v, n] * qs[n] for n in range(8)]
                 di = [e_ref[v, n] * qi[n] for n in range(8)]
                 while len(ds) > 1:
@@ -162,20 +173,23 @@
                 w_ref[8 * v : 8 * v + 8, :rank] -= ds[0]
                 w_ref[8 * v : 8 * v + 8, rank:] -= di[0]
 
-        def run(lo, hi):
+        def run(lo, hi, first, last):
             def body(b, _):
-                step(b, lo)
+                step(b, first, last)
                 return 0
 
             lax.fori_loop(lo, hi, body, 0)
 
-        run(0, 8)
-        run(8, 16)
-        inv_ref[...] = dot_t0(li_ref[...], li_ref[...], precision=HI)
+        half, end = rank // 16, rank // 8
+        mid = rank // 2
+        run(0, half // 2, 0, half)
+        run(half // 2, half, half // 2, half)
+        w_ref[mid:, :] = w_ref[mid:, :] - dot_t0(li_ref[:mid, mid:rank], li_ref[:mid, :], precision=HI)
+        run(half, half + half // 2, half, end)
+        run(half + half // 2, end, half + half // 2, end)
+        inv_ref[...] = dot_t0(li_ref[:, rank:], li_ref[:, rank:], precision=HI)
 
     cps = gather_b(0)
-    for cp in cps:
-        cp.start()
 
     lax.fori_loop(first, kk, load, 0)
     gather_and_u(0, cps)
@@ -253,8 +267,6 @@
         b_own = jnp.transpose(jnp.dot(inv_ref[...], mtt_b, precision=HI, preferred_element_type=F32))
         bcols[s + 1, w, t] = b_own.astype(BF16)
         gcs = gather_b(s + 1)
-        for cp in gcs:
-            cp.start()
         out[ii // 4 : ii // 4 + rank, :] = b_own
 
         gather_and_u(s + 1, gcs)
@@ -343,7 +355,7 @@
                 pltpu.VMEM((kk, rank, rank), F32),
                 pltpu.VMEM((rank, 2 * rank), F32),
                 pltpu.VMEM((rank // 8, 8, 8, rank), F32),
-                pltpu.VMEM((rank, rank), F32),
+                pltpu.VMEM((rank, 2 * rank), F32),
                 pltpu.VMEM((rank, rank), F32),
                 pltpu.VMEM((rank, rank), F32),
                 pltpu.VMEM((rank, rank), F32),

time: 81.7 us -> 76.9 us (0.941)
  Pallas kernels: 79.4 us -> 74.6 us
    pallas_call x1, Pallas kernels: 78.7 us -> 74 us  [local_sweeps(): pl.pallas_call(kernel, name='als', out_shape=jax.ShapeDtypeStruct((arows...]
where the time goes in v4:
time: 76.9 us; the launch traced here: 76.8 us
  Pallas kernels  74.6 us (97%)
  between operations  1.29 us (2%)
  local copies, waits for them, and re-layouts  0.89 us (1%)
    pallas_call x1, Pallas kernels, local_sweeps(): pl.pallas_call(kernel, name='als', out_shape=jax.ShapeDtypeStruct((arows...  74 us

profile of v4, /device:TPU:0, one launch (start us, length us, event | category | flops | bytes accessed | tf_op | source)
XLA Modules:
  0.0 76.8 jit_solution(656177453706347286)
XLA Ops:
  1.3 74.0 %als.1.src = f32[224,128]{1,0:T(8,128)} custom-call(f32[16,256,1024]{2,1,0:T(8,128)} %x_hbm.1, f32[128,128]{1,0:T(8,128)} %b_hbm.1, f32[32,128]{1,0:T(8,128)} %c_hbm.1, f32[1,1]{1,0:T(1,128)} %bitcast.1.lam_ref), custom_call_target="tpu_custom_call" | custom-call | tf_op jit(solution)/shard_map/als/pallas_call | solution.py:331
  75.2 0.0 copy-start
  75.3 0.9 %copy-done = f32[224,128]{1,0:T(8,128)S(1)} copy-done((f32[224,128]{1,0:T(8,128)S(1)}, f32[224,128]{1,0:T(8,128)}, u32[]{:S(2)}) %copy-start) | copy-done | bytes 114712
  76.1 0.6 results.1
Async XLA Ops:
  75.2 0.9 %copy-start = (f32[224,128]{1,0:T(8,128)S(1)}, f32[224,128]{1,0:T(8,128)}, u32[]{:S(2)}) copy-start(f32[224,128]{1,0:T(8,128)} %als.1.src) | copy-start | bytes 344068

commit v5 on v4

--- a/solution.py
+++ b/solution.py
@@ -13,6 +13,7 @@
 
 YZ = [(1, 1, 0, 0), (0, 1, 0, 0), (1, 0, 0, 0)]
 SAME_CORE = [(1, 0, 1, 0), (0, 0, 1, 0), (1, 0, 0, 0)]
+YZ_FAR = [(1, 1, 1, 0), (0, 1, 1, 0), (1, 0, 1, 0), (0, 0, 1, 0)]
 PARTNER = (0, 0, 0, 1)
 ALL = YZ + [(t, c, x, k) for x, k in ((1, 1), (1, 0), (0, 1)) for c in (1, 0) for t in (1, 0)]
 
@@ -217,11 +218,10 @@
         a_own = jnp.dot(mtt_a, inv_ref[...], precision=HI, preferred_element_type=F32)
         a16[s, w, g] = a_own.astype(BF16)
         af[s, g] = a_own
-        ga = [push(a16.at[s, w, g], a16.at[s, w, g], aga_s.at[s, n], aga_r.at[s, n], off) for n, off in enumerate(ALL)]
+        ga = [
+            push(a16.at[s, w, g], a16.at[s, w, g], aga_s.at[s, n], aga_r.at[s, n], off) for n, off in enumerate(YZ + YZ_FAR)
+        ]
         for cp in ga:
-            cp.start()
-        fa = [push(af.at[s, g], af.at[s, g], af_s.at[s, n], af_r.at[s, n], off) for n, off in enumerate(YZ)]
-        for cp in fa:
             cp.start()
         out[: a_own.shape[0], :] = a_own
 
@@ -231,6 +231,12 @@
             cb[k] = jnp.broadcast_to(ct[:, k : k + 1], (rank, rank))
         for cp in ga[:3]:
             cp.wait()
+
+        def hand_on(w2, n):
+            return push(a16.at[s, w2], a16.at[s, w2], aga_s.at[s, n], aga_r.at[s, n], PARTNER)
+
+        near = hand_on(w, 7)
+        near.start()
         at_ref[...] = jnp.transpose(a16[s, w].reshape(ii, rank))
 
         def chunk(wc):
@@ -245,6 +251,10 @@
             vp[n] = chunk(((xc + 1 - n) % 2) * 2 + (1 - core))
             vc.append(push(vp.at[n], vpr.at[s, n], vp_s.at[s, n], vp_r.at[s, n], (0, 0, 0, 1)))
             vc[n].start()
+        for cp in ga[3:]:
+            cp.wait()
+        far = hand_on((1 - xc) * 2 + core, 8)
+        far.start()
         rb = []
         for n in range(2):
             mine = chunk(((xc + 1 - n) % 2) * 2 + core)
@@ -256,8 +266,11 @@
                 m = len(rb)
                 rb.append(push(vo.at[n, dev(off)[0]], rsb.at[s, m], rsb_s.at[s, m], rsb_r.at[s, m], off))
                 rb[m].start()
-        for cp in ga[3:]:
-            cp.wait()
+        fa = [push(af.at[s, g], af.at[s, g], af_s.at[s, n], af_r.at[s, n], off) for n, off in enumerate(YZ)]
+        for cp in fa:
+            cp.start()
+        near.wait()
+        far.wait()
         aall = a16[s].reshape(4 * ii, rank)
         ga_ref[...] = dot_t0(aall, aall)
         factor(ga_ref[...] * gram_c)
@@ -361,7 +374,7 @@
                 pltpu.VMEM((rank, rank), F32),
                 pltpu.VMEM(c_full.shape, F32),
                 dma((kk,)), dma((2,)),
-                *sems(SWEEPS, 3), *sems(SWEEPS, 15), *sems(SWEEPS, 3), *sems(SWEEPS, 2), *sems(SWEEPS, 3),
+                *sems(SWEEPS, 3), *sems(SWEEPS, 9), *sems(SWEEPS, 3), *sems(SWEEPS, 2), *sems(SWEEPS, 3),
                 *sems(SWEEPS + 1, 7), *sems(SWEEPS + 1), *sems(SWEEPS, 15),
             ],
             compiler_params=pltpu.CompilerParams(

time: 76.9 us -> 75.6 us (0.983)
  Pallas kernels: 74.6 us -> 73.2 us
    pallas_call x1, Pallas kernels: 74 us -> 72.6 us  [local_sweeps(): pl.pallas_call(kernel, name='als', out_shape=jax.ShapeDtypeStruct((arows...]
where the time goes in v5:
time: 75.6 us; the launch traced here: 75.4 us
  Pallas kernels  73.2 us (97%)
  between operations  1.29 us (2%)
  local copies, waits for them, and re-layouts  0.89 us (1%)
    pallas_call x1, Pallas kernels, local_sweeps(): pl.pallas_call(kernel, name='als', out_shape=jax.ShapeDtypeStruct((arows...  72.6 us

profile of v5, /device:TPU:0, one launch (start us, length us, event | category | flops | bytes accessed | tf_op | source)
XLA Modules:
  0.0 75.4 jit_solution(14266745637218948580)
XLA Ops:
  1.3 72.6 %als.1.src = f32[224,128]{1,0:T(8,128)} custom-call(f32[16,256,1024]{2,1,0:T(8,128)} %x_hbm.1, f32[128,128]{1,0:T(8,128)} %b_hbm.1, f32[32,128]{1,0:T(8,128)} %c_hbm.1, f32[1,1]{1,0:T(1,128)} %bitcast.1.lam_ref), custom_call_target="tpu_custom_call" | custom-call | tf_op jit(solution)/shard_map/als/pallas_call | solution.py:344
  73.9 0.0 copy-start
  73.9 0.9 %copy-done = f32[224,128]{1,0:T(8,128)S(1)} copy-done((f32[224,128]{1,0:T(8,128)S(1)}, f32[224,128]{1,0:T(8,128)}, u32[]{:S(2)}) %copy-start) | copy-done | bytes 114712
  74.8 0.6 results.1
Async XLA Ops:
  73.9 0.9 %copy-start = (f32[224,128]{1,0:T(8,128)S(1)}, f32[224,128]{1,0:T(8,128)}, u32[]{:S(2)}) copy-start(f32[224,128]{1,0:T(8,128)} %als.1.src) | copy-start | bytes 344068

commit v6 on v5

--- a/solution.py
+++ b/solution.py
@@ -87,6 +87,10 @@
             cp.start()
         return cps
 
+    def gram_part(s, k):
+        bmat = jnp.concatenate([bcols[s, 2 * n + k].reshape(2 * rank, rank) for n in range(2)], axis=0)
+        return dot_t0(bmat, bmat)
+
     def relay_b(s, cps):
         fwd = []
         for n, off in reversed(list(enumerate(SAME_CORE))):
@@ -94,17 +98,21 @@
             fwd.append(b_copy(s, 4 + n, dev(off), PARTNER))
             fwd[-1].start()
         cps[3].wait()
+        gbp[...] = gram_part(s, core)
         for cp in fwd:
             cp.wait()
-
-    def gram_copy(s):
-        return push(gbp, gbr.at[s], gb_s.at[s], gb_r.at[s], (0, 1, 0, 0))
+        gbp[...] += gram_part(s, 1 - core)
+        for h in range(2):
+            gram_copy(s, h).start()
+
+    mid = rank // 2
+
+    def gram_copy(s, h):
+        part = pl.ds(h * mid, mid)
+        return push(gbp.at[part], gbr.at[s, part], gb_s.at[s, h], gb_r.at[s, h], (0, 1, 0, 0))
 
     def gather_and_u(s, cps):
         relay_b(s, cps)
-        bmat = bcols[s].reshape(jj, rank)
-        gbp[...] = dot_t0(bmat, bmat)
-        gram_copy(s).start()
 
         def body(k, _):
             acc = None
@@ -114,18 +122,24 @@
             u_ref[k] = acc
             return 0
 
-        lax.fori_loop(0, kk, body, 0, unroll=4)
-
-    def finish_gram_b(s):
-        gram_copy(s).wait()
-        gb_ref[...] = gbp[...] + gbr[s]
-
-    def factor(gram_prod):
+        lax.fori_loop(0, kk, body, 0, unroll=8)
+
+    def finish_gram_b(s, h):
+        part = pl.ds(h * mid, mid)
+        gram_copy(s, h).wait()
+        gb_ref[part, :] = gbp[part, :] + gbr[s, part, :]
+
+    def factor(gram_one, gram_two, ready=lambda h: None):
         rows = lax.broadcasted_iota(jnp.int32, (rank, rank), 0)
         cols = lax.broadcasted_iota(jnp.int32, (rank, rank), 1)
         eye = jnp.where(rows == cols, 1.0, 0.0).astype(F32)
-        w_ref[:, :rank] = gram_prod + lam_ref[0, 0] * eye
-        w_ref[:, rank:] = eye
+
+        def fill(h):
+            ready(h)
+            part = slice(h * mid, (h + 1) * mid)
+            w_ref[part, :rank] = gram_one[part, :] * gram_two[part, :] + lam_ref[0, 0] * eye[part, :]
+            w_ref[part, rank:] = eye[part, :]
+
         r1 = lax.broadcasted_iota(jnp.int32, (8, rank), 0)
 
         def lane(x, n):
@@ -182,19 +196,18 @@
             lax.fori_loop(lo, hi, body, 0)
 
         half, end = rank // 16, rank // 8
-        mid = rank // 2
+        fill(0)
         run(0, half // 2, 0, half)
         run(half // 2, half, half // 2, half)
+        fill(1)
         w_ref[mid:, :] = w_ref[mid:, :] - dot_t0(li_ref[:mid, mid:rank], li_ref[:mid, :], precision=HI)
         run(half, half + half // 2, half, end)
         run(half + half // 2, end, half + half // 2, end)
-        inv_ref[...] = dot_t0(li_ref[:, rank:], li_ref[:, rank:], precision=HI)
 
     cps = gather_b(0)
 
     lax.fori_loop(first, kk, load, 0)
     gather_and_u(0, cps)
-    finish_gram_b(0)
 
     def sweep(s, _):
         c16 = cfac[...].astype(BF16)
@@ -211,7 +224,14 @@
             ra.append(push(pa.at[g2], rsa.at[s, n], rsa_s.at[s, n], rsa_r.at[s, n], off))
         for cp in ra:
             cp.start()
-        factor(gb_ref[...] * gram_c)
+
+        def ready_first(h):
+            @pl.when(s == 0)
+            def _():
+                finish_gram_b(0, h)
+
+        factor(gb_ref, gram_c, ready_first)
+        inv_ref[...] = dot_t0(li_ref[:, rank:], li_ref[:, rank:], precision=HI)
         for cp in ra:
             cp.wait()
         mtt_a = pa[g] + rsa[s, 0] + rsa[s, 1] + rsa[s, 2]
@@ -273,7 +293,8 @@
         far.wait()
         aall = a16[s].reshape(4 * ii, rank)
         ga_ref[...] = dot_t0(aall, aall)
-        factor(ga_ref[...] * gram_c)
+        factor(ga_ref, gram_c)
+        inv_ref[...] = dot_t0(li_ref[:, rank:], li_ref[:, rank:], precision=HI)
         for cp in rb:
             cp.wait()
         mtt_b = vo[1, t] + rsb[s, 0] + rsb[s, 1] + rsb[s, 2]
@@ -292,8 +313,8 @@
         cs = [push(pc.at[s, me], pc.at[s, me], pc_s.at[s, n], pc_r.at[s, n], off) for n, off in enumerate(ALL)]
         for cp in cs:
             cp.start()
-        finish_gram_b(s + 1)
-        factor(ga_ref[...] * gb_ref[...])
+        factor(ga_ref, gb_ref, lambda h: finish_gram_b(s + 1, h))
+        inv_ref[...] = dot_t0(li_ref[:, rank:], li_ref[:, rank:], precision=HI)
         for cp in cs:
             cp.wait()
         halves = []
@@ -375,7 +396,7 @@
                 pltpu.VMEM(c_full.shape, F32),
                 dma((kk,)), dma((2,)),
                 *sems(SWEEPS, 3), *sems(SWEEPS, 9), *sems(SWEEPS, 3), *sems(SWEEPS, 2), *sems(SWEEPS, 3),
-                *sems(SWEEPS + 1, 7), *sems(SWEEPS + 1), *sems(SWEEPS, 15),
+                *sems(SWEEPS + 1, 7), *sems(SWEEPS + 1, 2), *sems(SWEEPS, 15),
             ],
             compiler_params=pltpu.CompilerParams(
                 collective_id=0, has_side_effects=True, vmem_limit_bytes=56 * 1024 * 1024

time: 75.6 us -> 73.8 us (0.976)
  Pallas kernels: 73.2 us -> 71.5 us
    pallas_call x1, Pallas kernels: 72.6 us -> 70.8 us  [local_sweeps(): pl.pallas_call(kernel, name='als', out_shape=jax.ShapeDtypeStruct((arows...]
where the time goes in v6:
time: 73.8 us; the launch traced here: 73.6 us
  Pallas kernels  71.5 us (97%)
  between operations  1.29 us (2%)
  local copies, waits for them, and re-layouts  0.89 us (1%)
    pallas_call x1, Pallas kernels, local_sweeps(): pl.pallas_call(kernel, name='als', out_shape=jax.ShapeDtypeStruct((arows...  70.8 us

profile of v6, /device:TPU:0, one launch (start us, length us, event | category | flops | bytes accessed | tf_op | source)
XLA Modules:
  0.0 73.6 jit_solution(5062690955084483290)
XLA Ops:
  1.3 70.8 %als.1.src = f32[224,128]{1,0:T(8,128)} custom-call(f32[16,256,1024]{2,1,0:T(8,128)} %x_hbm.1, f32[128,128]{1,0:T(8,128)} %b_hbm.1, f32[32,128]{1,0:T(8,128)} %c_hbm.1, f32[1,1]{1,0:T(1,128)} %bitcast.1.lam_ref), custom_call_target="tpu_custom_call" | custom-call | tf_op jit(solution)/shard_map/als/pallas_call | solution.py:365
  72.1 0.0 copy-start
  72.1 0.9 %copy-done = f32[224,128]{1,0:T(8,128)S(1)} copy-done((f32[224,128]{1,0:T(8,128)S(1)}, f32[224,128]{1,0:T(8,128)}, u32[]{:S(2)}) %copy-start) | copy-done | bytes 114712
  73.0 0.6 results.1
Async XLA Ops:
  72.1 0.9 %copy-start = (f32[224,128]{1,0:T(8,128)S(1)}, f32[224,128]{1,0:T(8,128)}, u32[]{:S(2)}) copy-start(f32[224,128]{1,0:T(8,128)} %als.1.src) | copy-start | bytes 344068

commit v7 on v6

--- a/solution.py
+++ b/solution.py
@@ -23,9 +23,9 @@
 
 
 def kernel(
-    x_hbm, b_hbm, c_hbm, lam_ref,
+    x_hbm, b_hbm, c_hbm, lam_hbm,
     out,
-    xf, xh, u_ref, b_in, bcols, a16, at_ref, af, pa, rsa, vp, vpr, vo, rsb, gbp, gbr, pc, cb,
+    lam_ref, xf, xh, u_ref, b_in, bcols, a16, at_ref, af, pa, rsa, vp, vpr, vo, rsb, gbp, gbr, pc, cb,
     w_ref, e_ref, li_ref, inv_ref, ga_ref, gb_ref, cfac,
     x_sem, in_sem, rsa_s, rsa_r, aga_s, aga_r, af_s, af_r, vp_s, vp_r, rsb_s, rsb_r, agb_s, agb_r, gb_s, gb_r, pc_s, pc_r,
 ):
@@ -41,6 +41,7 @@
     ins = [
         pltpu.make_async_copy(b_hbm, b_in, in_sem.at[0]),
         pltpu.make_async_copy(c_hbm, cfac, in_sem.at[1]),
+        pltpu.make_async_copy(lam_hbm, lam_ref, in_sem.at[2]),
     ]
     for cp in ins:
         cp.start()
@@ -65,8 +66,7 @@
     barrier = pltpu.get_barrier_semaphore()
     for off in reversed(ALL):
         pl.semaphore_signal(barrier, inc=1, device_id=dev(off), device_id_type=MESH)
-    for cp in ins:
-        cp.wait()
+    ins[0].wait()
     bcols[0, w, t] = b_in[...].astype(BF16)
     first = 4
     lax.fori_loop(0, first, load, 0)
@@ -207,6 +207,8 @@
     cps = gather_b(0)
 
     lax.fori_loop(first, kk, load, 0)
+    for cp in ins[1:]:
+        cp.wait()
     gather_and_u(0, cps)
 
     def sweep(s, _):
@@ -365,10 +367,11 @@
         packed = pl.pallas_call(
             kernel,
             name="als",
-            out_shape=jax.ShapeDtypeStruct((arows + brows + crows, rank), F32),
-            in_specs=[hbm, hbm, hbm, pl.BlockSpec(memory_space=pltpu.SMEM)],
+            out_shape=pltpu.VMEM((arows + brows + crows, rank), F32),
+            in_specs=[hbm] * 4,
             out_specs=vmem,
             scratch_shapes=[
+                pltpu.SMEM((1, 1), F32),
                 pltpu.VMEM((kk, ii, jj), F32),
                 pltpu.VMEM((kk, jj // ii, ii, ii), BF16),
                 pltpu.VMEM((kk, ii, rank), F32),
@@ -394,7 +397,7 @@
                 pltpu.VMEM((rank, rank), F32),
                 pltpu.VMEM((rank, rank), F32),
                 pltpu.VMEM(c_full.shape, F32),
-                dma((kk,)), dma((2,)),
+                dma((kk,)), dma((3,)),
                 *sems(SWEEPS, 3), *sems(SWEEPS, 9), *sems(SWEEPS, 3), *sems(SWEEPS, 2), *sems(SWEEPS, 3),
                 *sems(SWEEPS + 1, 7), *sems(SWEEPS + 1, 2), *sems(SWEEPS, 15),
             ],

time: 73.8 us -> 71.9 us (0.974)
  Pallas kernels: 71.5 us -> 70.5 us
  local copies, waits for them, and re-layouts: 0.89 us -> 0 us
    pallas_call x1, Pallas kernels: 70.8 us -> 69.9 us  [local_sweeps(): pl.pallas_call(kernel, name='als', out_shape=pltpu.VMEM((arows + brows +...]
    unnamed x2 -> x0, local copies, waits for them, and re-layouts: 0.89 us -> none
where the time goes in v7:
time: 71.9 us; the launch traced here: 71.8 us
  Pallas kernels  70.5 us (98%)
  between operations  1.29 us (2%)
    pallas_call x1, Pallas kernels, local_sweeps(): pl.pallas_call(kernel, name='als', out_shape=pltpu.VMEM((arows + brows +...  69.9 us

profile of v7, /device:TPU:0, one launch (start us, length us, event | category | flops | bytes accessed | tf_op | source)
XLA Modules:
  0.0 71.8 jit_solution(10940563547679766057)
XLA Ops:
  1.3 69.9 %als.1.src = f32[224,128]{1,0:T(8,128)S(1)} custom-call(f32[16,256,1024]{2,1,0:T(8,128)} %x_hbm.1, f32[128,128]{1,0:T(8,128)} %b_hbm.1, f32[32,128]{1,0:T(8,128)} %c_hbm.1, f32[1,1]{1,0:T(1,128)} %bitcast.1.lam_hbm), custom_call_target="tpu_custom_call" | custom-call | tf_op jit(solution)/shard_map/als/pallas_call | solution.py:367
  71.2 0.6 results.1

commit v8 on v7

--- a/solution.py
+++ b/solution.py
@@ -111,7 +111,7 @@
         part = pl.ds(h * mid, mid)
         return push(gbp.at[part], gbr.at[s, part], gb_s.at[s, h], gb_r.at[s, h], (0, 1, 0, 0))
 
-    def gather_and_u(s, cps):
+    def gather_and_u(s, cps, each=lambda k, u: None):
         relay_b(s, cps)
 
         def body(k, _):
@@ -120,6 +120,7 @@
                 p = jnp.dot(xh[k, n], bcols[s, n].reshape(2 * rank, rank), preferred_element_type=F32)
                 acc = p if acc is None else acc + p
             u_ref[k] = acc
+            each(k, acc)
             return 0
 
         lax.fori_loop(0, kk, body, 0, unroll=8)
@@ -215,17 +216,21 @@
         c16 = cfac[...].astype(BF16)
         gram_c = dot_t0(c16, c16)
 
-        def body_a(k, acc):
-            return acc + u_ref[k] * cfac[pl.ds(t * kk + k, 1), :]
-
-        part = lax.fori_loop(0, kk, body_a, jnp.zeros((ii, rank), F32))
-        pa[...] = part.reshape(pa.shape)
+        def sum_rows(g2):
+            part = pl.ds(pl.multiple_of(g2 * pa.shape[1], 8), pa.shape[1])
+
+            def body(k, acc):
+                return acc + u_ref[k, part, :] * cfac[pl.ds(t * kk + k, 1), :]
+
+            pa[g2] = lax.fori_loop(0, kk, body, jnp.zeros(pa.shape[1:], F32), unroll=8)
+
         ra = []
         for n, off in enumerate(YZ):
             g2 = dev(off)[1] * 2 + dev(off)[0]
+            sum_rows(g2)
             ra.append(push(pa.at[g2], rsa.at[s, n], rsa_s.at[s, n], rsa_r.at[s, n], off))
-        for cp in ra:
-            cp.start()
+            ra[n].start()
+        sum_rows(g)
 
         def ready_first(h):
             @pl.when(s == 0)
@@ -305,13 +310,13 @@
         gcs = gather_b(s + 1)
         out[ii // 4 : ii // 4 + rank, :] = b_own
 
-        gather_and_u(s + 1, gcs)
         for cp in fa:
             cp.wait()
-        afull = af[s].reshape(ii, rank)
-        pc[s, me] = jnp.concatenate(
-            [jnp.sum(u_ref[k] * afull, axis=0, keepdims=True) for k in range(kk)], axis=0
-        )
+
+        def part_c(k, u):
+            pc[s, me, pl.ds(k, 1), :] = jnp.sum(u * af[s].reshape(ii, rank), axis=0, keepdims=True)
+
+        gather_and_u(s + 1, gcs, part_c)
         cs = [push(pc.at[s, me], pc.at[s, me], pc_s.at[s, n], pc_r.at[s, n], off) for n, off in enumerate(ALL)]
         for cp in cs:
             cp.start()

time: 71.9 us -> 71.4 us (level)
  no operation moved by 1% of the time
where the time goes in v8:
time: 71.4 us; the launch traced here: 71.3 us
  Pallas kernels  70 us (98%)
  between operations  1.29 us (2%)
    pallas_call x1, Pallas kernels, local_sweeps(): pl.pallas_call(kernel, name='als', out_shape=pltpu.VMEM((arows + brows +...  69.4 us

profile of v8, /device:TPU:0, one launch (start us, length us, event | category | flops | bytes accessed | tf_op | source)
XLA Modules:
  0.0 71.3 jit_solution(8850508935888453613)
XLA Ops:
  1.3 69.4 %als.1.src = f32[224,128]{1,0:T(8,128)S(1)} custom-call(f32[16,256,1024]{2,1,0:T(8,128)} %x_hbm.1, f32[128,128]{1,0:T(8,128)} %b_hbm.1, f32[32,128]{1,0:T(8,128)} %c_hbm.1, f32[1,1]{1,0:T(1,128)} %bitcast.1.lam_hbm), custom_call_target="tpu_custom_call" | custom-call | tf_op jit(solution)/shard_map/als/pallas_call | solution.py:372
  70.7 0.6 results.1

commit v9 on v8

--- a/solution.py
+++ b/solution.py
@@ -45,7 +45,7 @@
     ]
     for cp in ins:
         cp.start()
-    depth = 4
+    depth = 5
     for k in range(depth):
         pltpu.make_async_copy(x_hbm.at[k], xf.at[k], x_sem.at[k]).start()
 
@@ -130,7 +130,7 @@
         gram_copy(s, h).wait()
         gb_ref[part, :] = gbp[part, :] + gbr[s, part, :]
 
-    def factor(gram_one, gram_two, ready=lambda h: None):
+    def factor(gram_one, gram_two, ready=lambda h: None, by=4):
         rows = lax.broadcasted_iota(jnp.int32, (rank, rank), 0)
         cols = lax.broadcasted_iota(jnp.int32, (rank, rank), 1)
         eye = jnp.where(rows == cols, 1.0, 0.0).astype(F32)
@@ -198,12 +198,12 @@
 
         half, end = rank // 16, rank // 8
         fill(0)
-        run(0, half // 2, 0, half)
-        run(half // 2, half, half // 2, half)
+        for n in range(0, half, by):
+            run(n, n + by, n, half)
         fill(1)
         w_ref[mid:, :] = w_ref[mid:, :] - dot_t0(li_ref[:mid, mid:rank], li_ref[:mid, :], precision=HI)
-        run(half, half + half // 2, half, end)
-        run(half + half // 2, end, half + half // 2, end)
+        for n in range(half, end, by):
+            run(n, n + by, n, end)
 
     cps = gather_b(0)
 
@@ -237,7 +237,7 @@
             def _():
                 finish_gram_b(0, h)
 
-        factor(gb_ref, gram_c, ready_first)
+        factor(gb_ref, gram_c, ready_first, by=2)
         inv_ref[...] = dot_t0(li_ref[:, rank:], li_ref[:, rank:], precision=HI)
         for cp in ra:
             cp.wait()

time: 71.4 us -> 70.8 us (level)
  no operation moved by 1% of the time
where the time goes in v9:
time: 70.8 us; the launch traced here: 70.7 us
  Pallas kernels  69.4 us (98%)
  between operations  1.29 us (2%)
    pallas_call x1, Pallas kernels, local_sweeps(): pl.pallas_call(kernel, name='als', out_shape=pltpu.VMEM((arows + brows +...  68.8 us

profile of v9, /device:TPU:0, one launch (start us, length us, event | category | flops | bytes accessed | tf_op | source)
XLA Modules:
  0.0 70.7 jit_solution(17628329962270969920)
XLA Ops:
  1.3 68.8 %als.1.src = f32[224,128]{1,0:T(8,128)S(1)} custom-call(f32[16,256,1024]{2,1,0:T(8,128)} %x_hbm.1, f32[128,128]{1,0:T(8,128)} %b_hbm.1, f32[32,128]{1,0:T(8,128)} %c_hbm.1, f32[1,1]{1,0:T(1,128)} %bitcast.1.lam_hbm), custom_call_target="tpu_custom_call" | custom-call | tf_op jit(solution)/shard_map/als/pallas_call | solution.py:372
  70.1 0.6 results.1

commit v10 on v9

--- a/solution.py
+++ b/solution.py
@@ -320,7 +320,7 @@
         cs = [push(pc.at[s, me], pc.at[s, me], pc_s.at[s, n], pc_r.at[s, n], off) for n, off in enumerate(ALL)]
         for cp in cs:
             cp.start()
-        factor(ga_ref, gb_ref, lambda h: finish_gram_b(s + 1, h))
+        factor(ga_ref, gb_ref, lambda h: finish_gram_b(s + 1, h), by=2)
         inv_ref[...] = dot_t0(li_ref[:, rank:], li_ref[:, rank:], precision=HI)
         for cp in cs:
             cp.wait()

time: 70.8 us -> 70.7 us (level)
  no operation moved by 1% of the time
where the time goes in v10:
time: 70.7 us; the launch traced here: 70.6 us
  Pallas kernels  69.3 us (98%)
  between operations  1.29 us (2%)
    pallas_call x1, Pallas kernels, local_sweeps(): pl.pallas_call(kernel, name='als', out_shape=pltpu.VMEM((arows + brows +...  68.6 us

profile of v10, /device:TPU:0, one launch (start us, length us, event | category | flops | bytes accessed | tf_op | source)
XLA Modules:
  0.0 70.6 jit_solution(5194580590387387329)
XLA Ops:
  1.3 68.6 %als.1.src = f32[224,128]{1,0:T(8,128)S(1)} custom-call(f32[16,256,1024]{2,1,0:T(8,128)} %x_hbm.1, f32[128,128]{1,0:T(8,128)} %b_hbm.1, f32[32,128]{1,0:T(8,128)} %c_hbm.1, f32[1,1]{1,0:T(1,128)} %bitcast.1.lam_hbm), custom_call_target="tpu_custom_call" | custom-call | tf_op jit(solution)/shard_map/als/pallas_call | solution.py:372
  69.9 0.6 results.1
